TPU v7x, 32 devices: a whole 2x2x4 slice. The times are simulated.
32 devices in a mesh: tm: 8 (over y, x, core), batch: 4 (over z).
Axes of the slice: x: 2, y: 2, z: 4, core: 2. Of those that a mesh axis runs over, the one named last changes fastest.
Arguments:
- hidden_states: bfloat16 [4, 1024, 5120], P('batch', 'tm'), may hold values from -6 to 6
- gen_weight: bfloat16 [64, 5120], replicated, may hold values from -0.078125 to 0.078125
- noise_field: bfloat16 [4, 64, 1024], P('batch', None, 'tm'), may hold values from -6 to 6
- timesteps: int32 [4], P('batch'), may hold values from 200 to 999
- embed_real: bfloat16 [128, 5120], replicated, may hold values from -0.5 to 0.5
- time_real: bfloat16 [256, 3, 5120], P('tm'), may hold values from -0.375 to 0.375
- query_real: bfloat16 [5120, 1024], P(None, 'tm'), may hold values from -3 to 3
- key_real: bfloat16 [5120, 1024], P(None, 'tm'), may hold values from -3 to 3
- value_real: bfloat16 [5120, 1024], P(None, 'tm'), may hold values from -0.078125 to 0.078125
- out_real: bfloat16 [1024, 5120], P('tm'), may hold values from -0.1875 to 0.1875
- gain_real: float32 [2, 1024], P(None, 'tm'), may hold values from 0.25 to 3
- proj_real: bfloat16 [64, 5120], replicated, may hold values from -0.078125 to 0.078125
- embed_fake: bfloat16 [128, 5120], replicated, may hold values from -0.5 to 0.5
- time_fake: bfloat16 [256, 3, 5120], P('tm'), may hold values from -0.375 to 0.375
- query_fake: bfloat16 [5120, 1024], P(None, 'tm'), may hold values from -3 to 3
- key_fake: bfloat16 [5120, 1024], P(None, 'tm'), may hold values from -3 to 3
- value_fake: bfloat16 [5120, 1024], P(None, 'tm'), may hold values from -0.078125 to 0.078125
- out_fake: bfloat16 [1024, 5120], P('tm'), may hold values from -0.1875 to 0.1875
- gain_fake: float32 [2, 1024], P(None, 'tm'), may hold values from 0.25 to 3
- proj_fake: bfloat16 [64, 5120], replicated, may hold values from -0.078125 to 0.078125
Outputs:
- dmd_gradient: float32 [4, 64, 1024], P('batch', None, 'tm')
- weight_grad: float32 [64, 5120], replicated
All inputs are finite; a program needn't handle non-finite values.
Results may differ from a plain program's by a relative error of at most 0.019.
Values may be sent and summed in bfloat16 or wider, within the bound.
A program may use at most 128 MiB of HBM per device.

v0:
```python
import functools
import math

import jax
import jax.numpy as jnp
from jax import lax
from jax.experimental import pallas as pl
from jax.experimental.pallas import tpu as pltpu
from jax.sharding import PartitionSpec as P

HD = 128
FREQ = 256
FTOK = 128


norm_floor = 0.05
gap_floor = 0.25
highest = lax.Precision.HIGHEST


MESH = pl.DeviceIdType.MESH
f32 = jnp.float32
bf16 = jnp.bfloat16


def hail(sizes):
    barrier = pltpu.get_barrier_semaphore()
    for axis, size in sizes.items():
        me = lax.axis_index(axis)
        for k in range(1, size):
            pl.semaphore_signal(
                barrier, inc=1, device_id={axis: lax.rem(me + k, size)}, device_id_type=MESH
            )


def meet(sizes):
    count = sum(size - 1 for size in sizes.values())
    pl.semaphore_wait(pltpu.get_barrier_semaphore(), count)


def exchange(axis, size, source, slots, send, recv):
    me = lax.axis_index(axis)
    copies = []
    for k in range(1, size):
        peer = lax.rem(me + k, size)
        copy = pltpu.make_async_remote_copy(
            src_ref=source(peer),
            dst_ref=slots.at[me],
            send_sem=send.at[k],
            recv_sem=recv.at[k],
            device_id={axis: peer},
            device_id_type=MESH,
        )
        copy.start()
        copies.append(copy)
    return copies


def landed(copies):
    for copy in copies:
        copy.wait_recv()


def gone(copies):
    for copy in copies:
        copy.wait_send()


def sems(*sizes):
    return [pltpu.SemaphoreType.DMA((size,)) for size in sizes for _ in range(2)]


def split(wide):
    high = wide.astype(bf16)
    return high, (wide - high.astype(f32)).astype(bf16)


def dot_nt(left, right):
    return lax.dot_general(left, right, (((1,), (1,)), ((), ())), preferred_element_type=f32)


def dot(left, right):
    return jnp.dot(left, right, preferred_element_type=f32)


def main_kernel(n, nb, part, level_ref, wave_ref, noise_ref, gain_real, gain_fake, *refs):
    big, refs = refs[:16], refs[16:]
    (difference_ref, norm_ref, weight_ref), refs = refs[:3], refs[3:]
    held, refs = refs[:16], refs[16:]
    (load_sem, patches, parts, modul, fold, gate_fold, gram, inner, stack, qkv, squares,
     square_parts, keys, terms, term_parts, gap, gaps, noisy_ref, share_ref, columns_held, rounded,
     all_rounded, mixed, quarters, merged, grad) = refs[:26]
    sem = refs[26:]
    me = lax.axis_index("tm")
    mine = lax.axis_index("batch")
    core, chip = lax.rem(me, 2), lax.div(me, 2)
    chips = n // 2
    patch_rows, frame = noisy_ref.shape
    level = level_ref[0, 0]
    tokens = n * frame
    width = held[0].shape[1]
    chunks = width // part
    loads = []
    for i, (source, target) in enumerate(zip(big, held)):
        loads.append(pltpu.make_async_copy(source, target, load_sem.at[i]))
    for i in (13, 12, 14, 15, *range(12)):
        loads[i].start()
    nets = [held[6 * i : 6 * i + 6] for i in (0, 1)]
    hidden = held[12]

    hail({"tm": n, "batch": nb})
    loads[13].wait()
    loads[12].wait()
    made = dot_nt(held[13][...], hidden[...]).astype(bf16).astype(f32)
    noisy = ((1.0 - level) * made + level * noise_ref[...].astype(f32)).astype(bf16)
    noisy_ref[...] = noisy
    noisy = noisy.astype(f32)
    for i in (0, 1):
        loads[14 + i].wait()
        for j in range(3):
            share = dot(wave_ref[...], held[14 + i][j])
            for s in range(n):
                if s < chunks:
                    row = share[:1, s * part : (s + 1) * part]
                else:
                    row = jnp.zeros((1, part), f32)
                share_ref[s, 3 * i + j : 3 * i + j + 1] = row
    meet({"tm": n, "batch": nb})
    scatter = exchange("tm", n, lambda peer: share_ref.at[peer], parts, sem[0], sem[1])
    spread = exchange("tm", n, lambda peer: noisy_ref, patches, sem[2], sem[3])
    parts[me] = share_ref[me]
    patches[me] = noisy_ref[...]
    landed(scatter)
    modul[me] = jnp.sum(parts[...], axis=0)
    collect = exchange("tm", n, lambda peer: modul.at[me], modul, sem[4], sem[5])

    def columns(s):
        return pl.ds(pl.multiple_of(s * part, 128), part)

    def own_columns(peer):
        return hidden.at[:, columns(lax.rem(peer, chunks))]

    pass_hidden = exchange("tm", n, own_columns, columns_held, sem[10], sem[11])
    columns_held[me] = hidden[:, columns(lax.rem(me, chunks))]

    means = []
    for i, (embed, proj, query, key, value, out) in enumerate(nets):
        loads[6 * i].wait()
        loads[6 * i + 1].wait()
        mean = jnp.sum(embed[...].astype(f32), axis=1, keepdims=True) / width
        means.append(mean)
        gram[i] = jnp.zeros(gram.shape[1:], f32)
        inner[i] = jnp.zeros(inner.shape[1:], f32)

        def gram_step(s, carry):
            table = embed[:, columns(s)]
            high, low = split(table.astype(f32) - mean)
            own = dot_nt(high, high)
            cross = dot_nt(high, low)
            gram[i] += own + cross + cross.T
            inner[i] += dot_nt(proj[:, columns(s)], table)
            return carry

        lax.fori_loop(0, chunks, gram_step, 0)

    landed(spread)
    kin = 2 * patch_rows
    for s in range(n):
        at = slice(s * frame, (s + 1) * frame)
        now = patches[s]
        before = patches[s - 1] if s else jnp.zeros_like(now)
        both = jnp.concatenate([now, before], axis=0)
        stack[:kin, at] = both
        stack[kin:, at] = both
    landed(collect)

    head = qkv.shape[1] // 3
    for i, (embed, proj, query, key, value, out) in enumerate(nets):
        for j in range(2, 6):
            loads[6 * i + j].wait()
        mean = means[i]
        fold[...] = jnp.zeros_like(fold)
        gate_fold[i] = jnp.zeros(gate_fold.shape[1:], f32)

        def fold_step(s, carry):
            at = columns(s)
            rows = modul[s]
            shift, scale, gate = (rows[3 * i + j : 3 * i + j + 1] for j in range(3))
            high, low = split((embed[:, at].astype(f32) - mean) * (1.0 + scale))
            shift_high, shift_low = split(jnp.broadcast_to(shift, (16, part)))
            left = jnp.concatenate([high, low, shift_high, shift_low], axis=0)
            right = jnp.concatenate([query[at, :], key[at, :], value[at, :]], axis=1)
            fold[...] += dot(left, right)
            high, low = split(proj[:, at].astype(f32) * gate)
            gate_fold[i] += dot_nt(jnp.concatenate([high, low], axis=0), out[:, at])
            return carry

        lax.fori_loop(0, chunks, fold_step, 0)
        folded = (fold[:kin] + fold[kin : 2 * kin]).T
        offset = (fold[2 * kin : 2 * kin + 8] + fold[2 * kin + 16 : 2 * kin + 24]).T[:, :1]
        gram_pair = jnp.concatenate(split(gram[i] / width), axis=1)
        fold_pair = jnp.concatenate(split(folded), axis=1)

        for s in range(n):
            at = slice(s * frame, (s + 1) * frame)
            pair = stack[:, at]
            variance = jnp.sum(pair[:kin].astype(f32) * dot(gram_pair, pair), axis=0, keepdims=True)
            rscale = lax.rsqrt(jnp.maximum(variance, 0.0) + norm_floor)
            full = dot(fold_pair, pair) * rscale + offset
            qkv[i, :, at] = full
            for j in range(2):
                rows = full[j * head : (j + 1) * head]
                squares[2 * i + j : 2 * i + j + 1, at] = jnp.sum(rows * rows, axis=0, keepdims=True)

    sums = exchange("tm", n, lambda peer: squares, square_parts, sem[6], sem[7])
    square_parts[me] = squares[...]
    landed(sums)
    inverse = lax.rsqrt(jnp.sum(square_parts[...], axis=0) / (head * n) + norm_floor)

    block = 2 * frame
    groups = min(4, tokens // block)
    gains = [ref[0:1, :] * ref[1:2, :] for ref in (gain_real, gain_fake)]
    per_group = tokens // block // groups
    for i in range(2):
        for s in range(n):
            at = slice(s * frame, (s + 1) * frame)
            gained = qkv[i, head : 2 * head, at] * inverse[2 * i + 1 : 2 * i + 2, at]
            keys[i, at, :] = (gained.T * gains[i]).astype(bf16)
            qkv[i, :head, at] = qkv[i, :head, at] * inverse[2 * i : 2 * i + 1, at]
    fold_outs = [
        (gate_fold[i, :patch_rows] + gate_fold[i, patch_rows:]).astype(bf16) for i in range(2)
    ]
    for group in range(groups):
        length = (group + 1) * per_group * block

        def block_step(b, carry):
            at = pl.ds(pl.multiple_of(b * block, block), block)
            for i in range(2):
                query = qkv[i, :head, at].astype(bf16)
                scores = dot(keys[i, :length], query)
                low = (length - per_group * block)
                key_frame = (lax.broadcasted_iota(jnp.int32, (length - low, block), 0) + low) // frame
                query_frame = (
                    lax.broadcasted_iota(jnp.int32, (length - low, block), 1) + b * block
                ) // frame
                edge = jnp.where(key_frame <= query_frame, scores[low:], -1e30)
                if low:
                    scores = jnp.concatenate([scores[:low], edge], axis=0)
                else:
                    scores = edge
                peak = jnp.max(scores, axis=0, keepdims=True)
                powers = jnp.exp((scores - peak) * (1.0 / math.sqrt(HD)))
                total = jnp.sum(powers, axis=0, keepdims=True)
                values = qkv[i, 2 * head :, :length].astype(bf16)
                attended = dot(values, powers.astype(bf16)) / total
                term = dot(fold_outs[i], attended.astype(bf16)).astype(bf16)
                for j in range(2):
                    terms[2 * b + j, i * patch_rows : (i + 1) * patch_rows] = term[
                        :, j * frame : (j + 1) * frame
                    ]
            return carry

        if per_group == 1:
            block_step(group, 0)
        else:
            lax.fori_loop(group * per_group, (group + 1) * per_group, block_step, 0)

    give = exchange("tm", n, lambda peer: terms.at[peer], term_parts, sem[8], sem[9])
    term_parts[me] = terms[me]
    own = stack[:, pl.ds(pl.multiple_of(me * frame, frame), frame)]
    direct = [dot(jnp.concatenate(split(inner[i]), axis=1), own) for i in range(2)]
    landed(give)
    summed = jnp.sum(term_parts[...].astype(f32), axis=0)
    pred_real = noisy - level * (summed[:patch_rows] + direct[0])
    pred_fake = noisy - level * (summed[patch_rows:] + direct[1])
    difference = pred_fake - pred_real
    distance = jnp.abs(made - pred_real)
    distance = jnp.sum(jnp.sum(distance, axis=0, keepdims=True), axis=1, keepdims=True)
    gap[...] = jnp.broadcast_to(distance, gap.shape)
    rounded[...] = difference.astype(bf16)
    difference_copies = exchange("tm", n, lambda peer: rounded, all_rounded, sem[12], sem[13])
    gap_copies = exchange("tm", n, lambda peer: gap, gaps, sem[14], sem[15])
    gaps[me] = gap[...]
    all_rounded[me] = rounded[...]
    landed(pass_hidden)
    landed(difference_copies)
    total = dot(all_rounded[0], columns_held[0])
    for s in range(1, n):
        total = total + dot(all_rounded[s], columns_held[s])
    landed(gap_copies)
    normalizer = jnp.maximum(jnp.sum(gaps[...], axis=0) / (patch_rows * tokens), gap_floor)
    norm_ref[...] = normalizer
    difference_ref[...] = difference / normalizer[:1, :1]
    total = total / normalizer[:1, :1] / math.sqrt(nb * tokens)
    mixed[...] = total.reshape(mixed.shape).astype(bf16)
    across = exchange("batch", nb, lambda peer: mixed.at[peer], quarters, sem[16], sem[17])
    quarters[mine] = mixed[mine]
    landed(across)
    merged[mine] = jnp.sum(quarters[...].astype(f32), axis=0).astype(bf16)
    back = exchange("batch", nb, lambda peer: merged.at[mine], merged, sem[18], sem[19])

    grad[core, chip, mine] = merged[mine]
    chain = []

    def to_chips(piece, k):
        copies = []
        for hop in range(1, chips):
            peer = lax.rem(chip + hop, chips)
            copy = pltpu.make_async_remote_copy(
                src_ref=merged.at[piece],
                dst_ref=grad.at[core, chip, piece],
                send_sem=sem[20].at[k * chips + hop],
                recv_sem=sem[21].at[k * chips + hop],
                device_id={"tm": 2 * peer + core},
                device_id_type=MESH,
            )
            copy.start()
            copies.append(copy)
        return copies

    chain.append(to_chips(mine, 0))
    for k in range(1, nb):
        back[k - 1].wait_recv()
        piece = lax.rem(mine + nb - k, nb)
        grad[core, chip, piece] = merged[piece]
        chain.append(to_chips(piece, k))

    def to_partner(at, hop):
        copy = pltpu.make_async_remote_copy(
            src_ref=grad.at[core, at],
            dst_ref=grad.at[core, at],
            send_sem=sem[22].at[hop],
            recv_sem=sem[23].at[hop],
            device_id={"tm": me + 1 - 2 * core},
            device_id_type=MESH,
        )
        copy.start()
        return copy

    shares = [to_partner(chip, 0)]
    for hop in range(1, chips):
        for copies in chain:
            copies[hop - 1].wait_recv()
        shares.append(to_partner(lax.rem(chip + chips - hop, chips), hop))
    landed(shares)
    for s in range(chunks):
        piece = grad[s % 2, s // 2]
        weight_ref[:, s * part : (s + 1) * part] = piece.reshape(patch_rows, part)
    for copies in (
        scatter, spread, collect, pass_hidden, sums, give, difference_copies, gap_copies,
        across, back, *chain, shares,
    ):
        gone(copies)


def sinusoid(time_step):
    half_freq = FREQ // 2
    frequency = jnp.exp(-math.log(10000.0) * jnp.arange(half_freq, dtype=jnp.float32) / half_freq)
    angles = time_step.astype(jnp.float32) * frequency
    return jnp.concatenate([jnp.cos(angles), jnp.sin(angles)]).astype(jnp.bfloat16)


def per_device(
    hidden_states,
    gen_weight,
    noise_field,
    timesteps,
    embed_real,
    time_real,
    query_real,
    key_real,
    value_real,
    out_real,
    gain_real,
    proj_real,
    embed_fake,
    time_fake,
    query_fake,
    key_fake,
    value_fake,
    out_fake,
    gain_fake,
    proj_fake,
):
    devices = lax.axis_size("tm")
    frame_tokens = hidden_states.shape[1]
    tokens = frame_tokens * devices
    patch_rows = gen_weight.shape[0]
    time_step = timesteps[0]
    level_raw = time_step.astype(jnp.float32) / 1000.0
    noise_level = 5.0 * level_raw / (1.0 + 4.0 * level_raw)
    sinus_wave = sinusoid(time_step)
    freq_rows = time_real.shape[0]
    own_wave = lax.dynamic_slice_in_dim(sinus_wave, lax.axis_index("tm") * freq_rows, freq_rows, 0)
    model_width = hidden_states.shape[2]
    batches = lax.axis_size("batch")
    part = -(-model_width // (devices * 128)) * 128
    while model_width % part:
        part += 128
    n, chips, quarter, head = devices, devices // 2, patch_rows // batches, query_real.shape[1]
    kin = 2 * patch_rows
    big = (
        embed_real, proj_real, query_real, key_real, value_real, out_real,
        embed_fake, proj_fake, query_fake, key_fake, value_fake, out_fake,
        hidden_states[0], gen_weight,
        time_real.transpose(1, 0, 2), time_fake.transpose(1, 0, 2),
    )
    vm = pltpu.VMEM
    scratch = [
        *[vm(array.shape, array.dtype) for array in big],
        pltpu.SemaphoreType.DMA((len(big),)),
        vm((n, patch_rows, frame_tokens), bf16),
        vm((n, 6, part), f32),
        vm((n, 6, part), f32),
        vm((2 * kin + 32, 3 * head), f32),
        vm((2, kin, head), f32),
        vm((2, kin, kin), f32),
        vm((2, patch_rows, kin), f32),
        vm((2 * kin, tokens), bf16),
        vm((2, 3 * head, tokens), f32),
        vm((4, tokens), f32),
        vm((n, 4, tokens), f32),
        vm((2, tokens, head), bf16),
        vm((n, kin, frame_tokens), bf16),
        vm((n, kin, frame_tokens), bf16),
        vm((8, 128), f32),
        vm((n, 8, 128), f32),
        vm((patch_rows, frame_tokens), bf16),
        vm((n, 6, part), f32),
        vm((n, frame_tokens, part), bf16),
        vm((patch_rows, frame_tokens), bf16),
        vm((n, patch_rows, frame_tokens), bf16),
        vm((batches, quarter, part), bf16),
        vm((batches, quarter, part), bf16),
        vm((batches, quarter, part), bf16),
        vm((2, chips, batches, quarter, part), bf16),
        *sems(n, n, n, n, n, n, n, n, batches, batches, batches * chips, chips),
    ]
    vmem = pl.BlockSpec(memory_space=pltpu.VMEM)
    difference, norm, weight_grad = pl.pallas_call(
        functools.partial(main_kernel, devices, batches, part),
        out_shape=[
            jax.ShapeDtypeStruct((patch_rows, frame_tokens), f32),
            jax.ShapeDtypeStruct((8, 128), f32),
            jax.ShapeDtypeStruct((patch_rows, model_width), bf16),
        ],
        in_specs=[pl.BlockSpec(memory_space=pltpu.SMEM)] + [vmem] * 4 + [pl.BlockSpec(memory_space=pl.ANY)] * len(big),
        out_specs=[vmem] * 3,
        scratch_shapes=scratch,
        compiler_params=pltpu.CompilerParams(
            collective_id=0, has_side_effects=True, vmem_limit_bytes=60 * 1024 * 1024
        ),
    )(
        noise_level.reshape(1, 1),
        jnp.broadcast_to(own_wave, (16, freq_rows)),
        noise_field[0],
        gain_real,
        gain_fake,
        *big,
    )
    return (difference[None], weight_grad.astype(f32))


def solution(mesh):
    in_specs = (
        P("batch", "tm", None),
        P(),
        P("batch", None, "tm"),
        P("batch"),
        P(),
        P("tm", None, None),
        P(None, "tm"),
        P(None, "tm"),
        P(None, "tm"),
        P("tm", None),
        P(None, "tm"),
        P(),
        P(),
        P("tm", None, None),
        P(None, "tm"),
        P(None, "tm"),
        P(None, "tm"),
        P("tm", None),
        P(None, "tm"),
        P(),
    )
    out_specs = (P("batch", None, "tm"), P())
    return jax.shard_map(
        per_device, mesh=mesh, in_specs=in_specs, out_specs=out_specs, check_vma=False
    )
```

profile of v0, /device:TPU:0, one launch (start us, length us, event | category | flops | bytes accessed | tf_op | source)
XLA Modules:
  0.0 66.9 jit_solution(16807742316200290216)
XLA Ops:
  1.3 0.1 sine_convert_fusion
  1.4 0.1 dynamic_slice.3
  1.5 0.6 broadcast_in_dim.6.wave_ref
  2.1 62.0 %shard_map.203 = (f32[64,128]{1,0:T(8,128)}, f32[8,128]{1,0:T(8,128)}, bf16[64,5120]{1,0:T(8,128)(2,1)}) custom-call(f32[1,1]{1,0:T(1,128)} %bitcast.1.level_ref, bf16[16,32]{1,0:T(8,128)(2,1)} %broadcast_in_dim.6.wave_ref, bf16[64,128]{1,0:T(8,128)(2,1)} %bitcast.11, f32[2,128]{1,0:T(2,128)} %gain_real.1, f32[2,128]{1,0:T(2,128)} %gain_fake.1, ...), custom_call_target="tpu_custom_call" | custom-call | tf_op jit(solution)/shard_map/pallas_call | solution.py:440
  64.0 0.0 copy-start
  64.1 2.2 %convert_element_type.13 = f32[64,5120]{1,0:T(8,128)} convert(bf16[64,5120]{1,0:T(8,128)(2,1)} %get-tuple-element.5) | non-fusion elementwise | flops 327680 | bytes 1966080 | tf_op jit(solution)/shard_map/convert_element_type | solution.py:461
  66.3 0.0 copy-done
  66.3 0.6 copy.24
  (1 shorter events, 0.0 us)
Async XLA Ops:
  64.0 2.2 %copy-start = (f32[64,128]{1,0:T(8,128)S(1)}, f32[64,128]{1,0:T(8,128)}, u32[]{:S(2)}) copy-start(f32[64,128]{1,0:T(8,128)} %get-tuple-element.4) | copy-start | bytes 98308
where the time goes:
time: 67.2 us; the launch traced here: 66.9 us
  Pallas kernels  62 us (92%)
  other arithmetic  2.29 us (3%)
  between operations  1.35 us (2%)
  local copies, waits for them, and re-layouts  1.3 us (2%)
    pallas_call x1, Pallas kernels, per_device(): pl.pallas_call(functools.partial(main_kernel, devices, batches, part), ou...  62 us
    convert_element_type x1, other arithmetic, per_device(): return (difference[None], weight_grad.astype(f32))  2.23 us

commit v1 on v0

v1 whole, which is shorter than its diff:
```python
import functools
import math

import jax
import jax.numpy as jnp
import numpy as np
from jax import lax
from jax.experimental import pallas as pl
from jax.experimental.pallas import tpu as pltpu
from jax.sharding import PartitionSpec as P

HD = 128
FREQ = 256

norm_floor = 0.05
gap_floor = 0.25

MESH = pl.DeviceIdType.MESH
f32 = jnp.float32
bf16 = jnp.bfloat16


def hail(sizes):
    barrier = pltpu.get_barrier_semaphore()
    for axis, size in sizes.items():
        me = lax.axis_index(axis)
        for k in range(1, size):
            pl.semaphore_signal(
                barrier, inc=1, device_id={axis: lax.rem(me + k, size)}, device_id_type=MESH
            )


def meet(sizes):
    count = sum(size - 1 for size in sizes.values())
    pl.semaphore_wait(pltpu.get_barrier_semaphore(), count)


def partner(me, k, size):
    if size & (size - 1):
        return lax.rem(me + k, size)
    peer, bit = me, 1
    while bit < size:
        if k & bit:
            peer = peer + bit - 2 * bit * lax.rem(lax.div(me, bit), 2)
        bit *= 2
    return peer


def exchange(axis, size, source, slots, send, recv, hops=None):
    me = lax.axis_index(axis)
    copies = []
    for k in hops or range(1, size):
        peer = partner(me, k, size)
        copy = pltpu.make_async_remote_copy(
            src_ref=source(peer),
            dst_ref=slots.at[me],
            send_sem=send.at[k],
            recv_sem=recv.at[k],
            device_id={axis: peer},
            device_id_type=MESH,
        )
        copy.start()
        copies.append(copy)
    return copies


def landed(copies):
    for copy in copies:
        copy.wait_recv()


def gone(copies):
    for copy in copies:
        copy.wait_send()


def split(wide):
    high = wide.astype(bf16)
    return high, (wide - high.astype(f32)).astype(bf16)


def dot_nt(left, right):
    return lax.dot_general(left, right, (((1,), (1,)), ((), ())), preferred_element_type=f32)


def dot(left, right):
    return jnp.dot(left, right, preferred_element_type=f32)


LOADS = (
    "timesteps", "freqs", "time0", "time1", "hidden", "gen", "noise", "embed0", "proj0", "embed1",
    "proj1", "query0", "key0", "query1", "key1", "value0", "out0", "value1", "out1", "gain0", "gain1",
)


def main_kernel(n, nb, part, step, names, *refs):
    r = dict(zip(names, refs, strict=True))
    me = lax.axis_index("tm")
    mine = lax.axis_index("batch")
    core, chip = lax.rem(me, 2), lax.div(me, 2)
    chips = n // 2
    hidden, stack, modul = r["v_hidden"], r["stack"], r["modul"]
    noisy_ref = r["noisy"]
    patch_rows, frame = noisy_ref.shape
    tokens = n * frame
    kin = 2 * patch_rows
    width = hidden.shape[1]
    chunks = width // part
    steps, merge = width // step, step // part
    head = r["v_query0"].shape[1]
    freq_rows = r["v_time0"].shape[1]
    loads = {}
    for i, name in enumerate(LOADS):
        loads[name] = pltpu.make_async_copy(r[name], r["v_" + name], r["load_sem"].at[i])
        loads[name].start()
    hail({"tm": n, "batch": nb})

    def sem(name):
        return r["s_" + name], r["r_" + name]

    loads["timesteps"].wait()
    loads["freqs"].wait()
    half = r["v_freqs"].shape[1]
    time_step = jnp.full((16, half), r["v_timesteps"][0], jnp.int32).astype(f32)
    angles = time_step * r["v_freqs"][...]
    wave = jnp.concatenate([jnp.cos(angles), jnp.sin(angles)], axis=1).astype(bf16)
    raw = time_step[:8] * (1.0 / 1000.0)
    level = ((5.0 * raw) / (1.0 + 4.0 * raw))[:1, :1]
    picked = (2 * half, 3 * freq_rows)
    column = lax.rem(lax.broadcasted_iota(jnp.int32, picked, 1), freq_rows) + me * freq_rows
    chosen = (lax.broadcasted_iota(jnp.int32, picked, 0) == column).astype(f32).astype(bf16)
    own_wave = dot(wave, chosen)
    block_of = lax.broadcasted_iota(jnp.int32, own_wave.shape, 1) // freq_rows
    row_of = lax.broadcasted_iota(jnp.int32, own_wave.shape, 0)
    share = None
    for i in (0, 1):
        loads[f"time{i}"].wait()
        table = r[f"v_time{i}"]
        left = jnp.where(row_of == block_of + 3 * i, own_wave, 0.0).astype(bf16)
        if freq_rows % 16:
            for j in range(3):
                term = dot(left[:, j * freq_rows : (j + 1) * freq_rows], table[j])
                share = term if share is None else share + term
        else:
            term = dot(left, table[...].reshape(3 * freq_rows, width))
            share = term if share is None else share + term
    share_ref, parts = r["share"], r["parts"]
    for s in range(n):
        if s < chunks:
            share_ref[s] = share[:8, s * part : (s + 1) * part].astype(share_ref.dtype)
        else:
            share_ref[s] = jnp.zeros((8, part), share_ref.dtype)
    meet({"tm": n, "batch": nb})
    scatter = exchange("tm", n, lambda peer: share_ref.at[peer], parts, *sem("scatter"))
    parts[me] = share_ref[me]

    loads["hidden"].wait()
    loads["gen"].wait()
    loads["noise"].wait()
    made = dot_nt(hidden[...], r["v_gen"][...]).T.astype(bf16).astype(f32)
    noisy = ((1.0 - level) * made + level * r["v_noise"][...].astype(f32)).astype(bf16)
    noisy_ref[...] = noisy
    patches = r["patches"]
    spread = exchange("tm", n, lambda peer: noisy_ref, patches, *sem("spread"))
    patches[me] = noisy_ref[...]
    noisy = noisy.astype(f32)

    def columns(s):
        return pl.ds(pl.multiple_of(s * part, 128), part)

    def wide(s):
        return pl.ds(pl.multiple_of(s * step, 128), step)

    columns_held = r["columns"]
    pass_hidden = []

    def pass_on(hops):
        hops = [k for k in hops if k < n]
        if hops:
            pass_hidden.extend(
                exchange(
                    "tm", n, lambda peer: hidden.at[:, columns(lax.rem(peer, chunks))],
                    columns_held, *sem("pass"), hops,
                )
            )

    pass_on([1])

    gram = r["gram"]
    extra = kin + patch_rows

    def gram_of(i):
        embed, proj = r[f"v_embed{i}"], r[f"v_proj{i}"]
        loads[f"embed{i}"].wait()
        loads[f"proj{i}"].wait()
        gram[i] = jnp.zeros(gram.shape[1:], f32)
        ones = jnp.ones((16, step), bf16)

        def gram_step(s, carry):
            table = embed[:, wide(s)]
            gram[i] += dot_nt(jnp.concatenate([table, proj[:, wide(s)], ones], axis=0), table)
            return carry

        lax.fori_loop(0, steps, gram_step, 0)

    gram_of(0)
    landed(scatter)
    modul[me] = jnp.sum(parts[...].astype(f32), axis=0).astype(modul.dtype)
    collect = exchange("tm", n, lambda peer: modul.at[me], modul, *sem("collect"))
    pass_on([2, 4])
    columns_held[me] = hidden[:, columns(lax.rem(me, chunks))]
    gram_of(1)

    landed(spread)
    for s in range(n):
        at = slice(s * frame, (s + 1) * frame)
        now = patches[s]
        before = patches[s - 1] if s else jnp.zeros_like(now)
        both = jnp.concatenate([now, before], axis=0)
        stack[:kin, at] = both
        stack[kin:, at] = both
    block = 2 * frame
    blocks = [slice(s * block, (s + 1) * block) for s in range(tokens // block)]
    rscale = r["rscale"]
    means = []
    for i in (0, 1):
        mean_row = gram[i, extra : extra + 8] / width
        means.append(mean_row.T[:, :1])
        centered = gram[i, :kin] / width - means[i] * mean_row[:1]
        gram_pair = jnp.concatenate(split(centered), axis=1)
        for at in blocks:
            pair = stack[:, at]
            variance = jnp.sum(pair[:kin].astype(f32) * dot(gram_pair, pair), axis=0, keepdims=True)
            rscale[i : i + 1, at] = lax.rsqrt(jnp.maximum(variance, 0.0) + norm_floor)
    landed(collect)
    pass_on([3, 5])

    left_ref, fold, fold_v, gate_fold = r["left"], r["fold"], r["fold_v"], r["gate_fold"]
    qk, squares, square_parts = r["qk"], r["squares"], r["square_parts"]

    def rows_of(s, first, count):
        found = [modul[s * merge + g].astype(f32)[first : first + count] for g in range(merge)]
        return found[0] if merge == 1 else jnp.concatenate(found, axis=1)

    def fold_qk(i):
        embed, query, key = r[f"v_embed{i}"], r[f"v_query{i}"], r[f"v_key{i}"]
        loads[f"query{i}"].wait()
        loads[f"key{i}"].wait()
        fold[i] = jnp.zeros(fold.shape[1:], f32)
        line = lax.broadcasted_iota(jnp.int32, (16, step), 0)

        def fold_step(s, carry):
            at = wide(s)
            rows = rows_of(s, 3 * i, 2)
            shift, scale = rows[:1], rows[1:2]
            high = ((embed[:, at].astype(f32) - means[i]) * (1.0 + scale)).astype(bf16)
            shift_high, shift_low = split(shift)
            shifts = jnp.where(
                line == 0, shift_high.astype(f32), jnp.where(line == 1, shift_low.astype(f32), 0.0)
            ).astype(bf16)
            left = jnp.concatenate([high, shifts], axis=0)
            left_ref[i, :, at] = left
            fold[i] += dot(left, jnp.concatenate([query[at, :], key[at, :]], axis=1))
            return carry

        lax.fori_loop(0, steps, fold_step, 0)
        folded = jnp.concatenate(split(fold[i, :kin].T), axis=1)
        tail = fold[i, kin : kin + 8].T
        offset = tail[:, :1] + tail[:, 1:2]
        for at in blocks:
            full = dot(folded, stack[:, at]) * rscale[i : i + 1, at] + offset
            qk[i, :, at] = full
            for j in range(2):
                rows = full[j * head : (j + 1) * head]
                squares[i, j : j + 1, at] = jnp.sum(rows * rows, axis=0, keepdims=True)
        copies = exchange(
            "tm", n, lambda peer: squares.at[i], square_parts.at[i], *sem(f"sums{i}")
        )
        square_parts[i, me] = squares[i]
        return copies

    values = r["values"]

    def fold_values(i):
        value, out, proj = r[f"v_value{i}"], r[f"v_out{i}"], r[f"v_proj{i}"]
        loads[f"value{i}"].wait()
        loads[f"out{i}"].wait()
        fold_v[i] = jnp.zeros(fold_v.shape[1:], f32)
        gate_fold[i] = jnp.zeros(gate_fold.shape[1:], f32)

        def value_step(s, carry):
            at = wide(s)
            gate = rows_of(s, 3 * i + 2, 1)
            fold_v[i] += dot(left_ref[i, :, at], value[at, :])
            gate_fold[i] += dot_nt(out[:, at], (proj[:, at].astype(f32) * gate).astype(bf16))
            return carry

        lax.fori_loop(0, steps, value_step, 0)
        gate_high, gate_low = split(gate_fold[i].T)
        value_high, value_low = split(fold_v[i])
        both = dot_nt(jnp.concatenate([gate_high, gate_low], axis=0), value_high)
        joint = both[:patch_rows] + both[patch_rows:] + dot_nt(gate_high, value_low)
        offset = joint[:, kin : kin + 1] + joint[:, kin + 1 : kin + 2]
        pairs = jnp.concatenate(split(joint[:, :kin]), axis=1)
        for at in blocks:
            full = dot(pairs, stack[:, at]) * rscale[i : i + 1, at] + offset
            values[i, :patch_rows, at] = full.astype(bf16)
            values[i, patch_rows:, at] = jnp.ones((16, block), bf16)

    sums = [fold_qk(0), fold_qk(1)]
    pass_on([6, 7, *range(8, n)])
    fold_values(0)
    fold_values(1)

    groups = min(4, tokens // block)
    per_group = tokens // block // groups
    keys, terms, term_parts = r["keys"], r["terms"], r["term_parts"]

    def attend(i):
        landed(sums[i])
        inverse = lax.rsqrt(jnp.sum(square_parts[i], axis=0) / (head * n) + norm_floor)
        gain = r[f"v_gain{i}"]
        gains = gain[0:1, :] * gain[1:2, :]
        to_query = math.log2(math.e) / math.sqrt(HD)
        for at in blocks:
            gained = qk[i, head:, at] * inverse[1:2, at]
            keys[i, at, :] = (gained.T * gains).astype(bf16)
            r["queries"][i, :, at] = (qk[i, :head, at] * (inverse[:1, at] * to_query)).astype(bf16)
        for group in range(groups):
            length = (group + 1) * per_group * block
            low = length - per_group * block

            def block_step(b, carry):
                at = pl.ds(pl.multiple_of(b * block, block), block)
                scores = dot(keys[i, :length], r["queries"][i, :, at])
                shape = (length - low, block)
                key_frame = (lax.broadcasted_iota(jnp.int32, shape, 0) + low) // frame
                query_frame = (lax.broadcasted_iota(jnp.int32, shape, 1) + b * block) // frame
                edge = jnp.where(key_frame <= query_frame, scores[low:], -1e30)
                scores = jnp.concatenate([scores[:low], edge], axis=0) if low else edge
                peak = jnp.max(scores, axis=0, keepdims=True)
                powers = jnp.exp2(scores - peak).astype(bf16)
                summed = dot(values[i, :, :length], powers)
                term = (summed[:patch_rows] / summed[patch_rows : patch_rows + 1]).astype(bf16)
                for j in range(2):
                    terms[i, 2 * b + j] = term[:, j * frame : (j + 1) * frame]
                return carry

            if per_group == 1:
                block_step(group, 0)
            else:
                lax.fori_loop(group * per_group, (group + 1) * per_group, block_step, 0)
        copies = exchange(
            "tm", n, lambda peer: terms.at[i, peer], term_parts.at[i], *sem(f"give{i}")
        )
        term_parts[i, me] = terms[i, me]
        return copies

    for name in ("gain0", "gain1"):
        loads[name].wait()
    give = [attend(0), attend(1)]

    own = stack[:, pl.ds(pl.multiple_of(me * frame, frame), frame)]
    velocity = []
    for i in (0, 1):
        inner = jnp.concatenate(split(gram[i, kin:extra]), axis=1)
        velocity.append(dot(inner, own))
    for i in (0, 1):
        landed(give[i])
        velocity[i] = velocity[i] + jnp.sum(term_parts[i].astype(f32), axis=0)
    pred_real = noisy - level * velocity[0]
    pred_fake = noisy - level * velocity[1]
    difference = pred_fake - pred_real
    rounded, all_rounded, gap, gaps = r["rounded"], r["all_rounded"], r["gap"], r["gaps"]
    rounded[...] = difference.astype(bf16)
    difference_copies = exchange("tm", n, lambda peer: rounded, all_rounded, *sem("diff"))
    distance = jnp.abs(made - pred_real)
    distance = jnp.sum(jnp.sum(distance, axis=0, keepdims=True), axis=1, keepdims=True)
    gap[...] = jnp.broadcast_to(distance, gap.shape)
    gap_copies = exchange("tm", n, lambda peer: gap, gaps, *sem("gap"))
    gaps[me] = gap[...]
    all_rounded[me] = rounded[...]
    landed(pass_hidden)
    landed(difference_copies)
    total = None
    for s in range(0, n, 2):
        lefts = jnp.concatenate([all_rounded[s], all_rounded[s + 1]], axis=1)
        term = dot(lefts, columns_held[s : s + 2].reshape(2 * frame, part))
        total = term if total is None else total + term
    landed(gap_copies)
    normalizer = jnp.maximum(jnp.sum(gaps[...], axis=0) / (patch_rows * tokens), gap_floor)
    r["difference"][...] = difference / normalizer[:1, :1]
    total = total * (1.0 / (normalizer[:1, :1] * math.sqrt(nb * tokens)))
    mixed, quarters, merged, grad = r["mixed"], r["quarters"], r["merged"], r["grad"]
    mixed[...] = total.reshape(mixed.shape).astype(bf16)
    across = exchange("batch", nb, lambda peer: mixed.at[peer], quarters, *sem("across"))
    quarters[mine] = mixed[mine]
    landed(across)
    merged[mine] = jnp.sum(quarters[...].astype(f32), axis=0).astype(bf16)
    back = exchange("batch", nb, lambda peer: merged.at[mine], merged, *sem("back"))

    grad[core, chip, mine] = merged[mine]
    chain = []

    def to_chips(piece, k):
        copies = []
        for hop in range(1, chips):
            peer = partner(chip, hop, chips)
            copy = pltpu.make_async_remote_copy(
                src_ref=merged.at[piece],
                dst_ref=grad.at[core, chip, piece],
                send_sem=r["s_chain"].at[k * chips + hop],
                recv_sem=r["r_chain"].at[k * chips + hop],
                device_id={"tm": 2 * peer + core},
                device_id_type=MESH,
            )
            copy.start()
            copies.append(copy)
        return copies

    chain.append(to_chips(mine, 0))
    for k in range(1, nb):
        back[k - 1].wait_recv()
        piece = partner(mine, k, nb)
        grad[core, chip, piece] = merged[piece]
        chain.append(to_chips(piece, k))

    def to_partner(at, hop):
        copy = pltpu.make_async_remote_copy(
            src_ref=grad.at[core, at],
            dst_ref=grad.at[core, at],
            send_sem=r["s_share"].at[hop],
            recv_sem=r["r_share"].at[hop],
            device_id={"tm": me + 1 - 2 * core},
            device_id_type=MESH,
        )
        copy.start()
        return copy

    shares = [to_partner(chip, 0)]
    for hop in range(1, chips):
        for copies in chain:
            copies[hop - 1].wait_recv()
        shares.append(to_partner(partner(chip, hop, chips), hop))
    landed(shares)
    weight_ref = r["weight"]
    for s in range(chunks):
        piece = grad[s % 2, s // 2]
        weight_ref[:, s * part : (s + 1) * part] = piece.reshape(patch_rows, part)
    for copies in (
        scatter, spread, collect, pass_hidden, *sums, *give, difference_copies, gap_copies,
        across, back, *chain, shares,
    ):
        gone(copies)


def per_device(
    hidden_states,
    gen_weight,
    noise_field,
    timesteps,
    embed_real,
    time_real,
    query_real,
    key_real,
    value_real,
    out_real,
    gain_real,
    proj_real,
    embed_fake,
    time_fake,
    query_fake,
    key_fake,
    value_fake,
    out_fake,
    gain_fake,
    proj_fake,
):
    n = lax.axis_size("tm")
    nb = lax.axis_size("batch")
    frame = hidden_states.shape[1]
    tokens = frame * n
    patch_rows, width = gen_weight.shape
    part = -(-width // (n * 128)) * 128
    while width % part:
        part += 128
    chunks = width // part
    merge = max(m for m in range(1, chunks + 1) if chunks % m == 0 and m * part <= 1280 or m == 1)
    step = merge * part
    chips, quarter, head = n // 2, patch_rows // nb, query_real.shape[1]
    kin = 2 * patch_rows
    half = FREQ // 2
    freqs = np.exp(-math.log(10000.0) * np.arange(half, dtype=np.float64) / half).astype(np.float32)
    inputs = dict(
        timesteps=timesteps, freqs=jnp.asarray(np.broadcast_to(freqs, (16, half))),
        time0=time_real.transpose(1, 0, 2), time1=time_fake.transpose(1, 0, 2),
        hidden=hidden_states[0], gen=gen_weight, noise=noise_field[0],
        embed0=embed_real, proj0=proj_real, embed1=embed_fake, proj1=proj_fake,
        query0=query_real, key0=key_real, query1=query_fake, key1=key_fake,
        value0=value_real, out0=out_real, value1=value_fake, out1=out_fake,
        gain0=gain_real, gain1=gain_fake,
    )
    vm = pltpu.VMEM
    outputs = dict(
        difference=jax.ShapeDtypeStruct((patch_rows, frame), f32),
        weight=jax.ShapeDtypeStruct((patch_rows, width), bf16),
    )
    scratch = {}
    for name in LOADS:
        array = inputs[name]
        scratch["v_" + name] = (pltpu.SMEM if name == "timesteps" else vm)(array.shape, array.dtype)
    scratch.update(
        load_sem=pltpu.SemaphoreType.DMA((len(LOADS),)),
        patches=vm((n, patch_rows, frame), bf16),
        share=vm((n, 8, part), bf16),
        parts=vm((n, 8, part), bf16),
        modul=vm((n, 8, part), bf16),
        noisy=vm((patch_rows, frame), bf16),
        columns=vm((n, frame, part), bf16),
        gram=vm((2, kin + patch_rows + 16, kin), f32),
        stack=vm((2 * kin, tokens), bf16),
        rscale=vm((2, tokens), f32),
        left=vm((2, kin + 16, width), bf16),
        fold=vm((2, kin + 16, 2 * head), f32),
        fold_v=vm((2, kin + 16, head), f32),
        gate_fold=vm((2, head, patch_rows), f32),
        qk=vm((2, 2 * head, tokens), f32),
        squares=vm((2, 2, tokens), f32),
        square_parts=vm((2, n, 2, tokens), f32),
        values=vm((2, patch_rows + 16, tokens), bf16),
        keys=vm((2, tokens, head), bf16),
        queries=vm((2, head, tokens), bf16),
        terms=vm((2, n, patch_rows, frame), bf16),
        term_parts=vm((2, n, patch_rows, frame), bf16),
        gap=vm((8, 128), f32),
        gaps=vm((n, 8, 128), f32),
        rounded=vm((patch_rows, frame), bf16),
        all_rounded=vm((n, patch_rows, frame), bf16),
        mixed=vm((nb, quarter, part), bf16),
        quarters=vm((nb, quarter, part), bf16),
        merged=vm((nb, quarter, part), bf16),
        grad=vm((2, chips, nb, quarter, part), bf16),
    )
    for name, count in dict(
        scatter=n, spread=n, collect=n, sums0=n, sums1=n, give0=n, give1=n, diff=n, gap=n,
        across=nb, back=nb, chain=nb * chips, share=chips,
    ).items():
        scratch["s_" + name] = pltpu.SemaphoreType.DMA((count,))
        scratch["r_" + name] = pltpu.SemaphoreType.DMA((count,))
    scratch["s_pass"] = pltpu.SemaphoreType.DMA((n,))
    scratch["r_pass"] = pltpu.SemaphoreType.DMA((n,))
    names = (*inputs, *outputs, *scratch)
    difference, weight_grad = pl.pallas_call(
        functools.partial(main_kernel, n, nb, part, step, names),
        out_shape=list(outputs.values()),
        in_specs=[pl.BlockSpec(memory_space=pl.ANY)] * len(inputs),
        out_specs=[pl.BlockSpec(memory_space=pltpu.VMEM)] * 2,
        scratch_shapes=list(scratch.values()),
        compiler_params=pltpu.CompilerParams(
            collective_id=0, has_side_effects=True, vmem_limit_bytes=60 * 1024 * 1024
        ),
    )(*inputs.values())
    return (difference[None], weight_grad.astype(f32))


def solution(mesh):
    in_specs = (
        P("batch", "tm", None),
        P(),
        P("batch", None, "tm"),
        P("batch"),
        P(),
        P("tm", None, None),
        P(None, "tm"),
        P(None, "tm"),
        P(None, "tm"),
        P("tm", None),
        P(None, "tm"),
        P(),
        P(),
        P("tm", None, None),
        P(None, "tm"),
        P(None, "tm"),
        P(None, "tm"),
        P("tm", None),
        P(None, "tm"),
        P(),
    )
    out_specs = (P("batch", None, "tm"), P())
    return jax.shard_map(
        per_device, mesh=mesh, in_specs=in_specs, out_specs=out_specs, check_vma=False
    )
```

time: 67.2 us -> 57.7 us (0.86)
  Pallas kernels: 62 us -> 52 us
    pallas_call x1, Pallas kernels: 62 us -> 52 us  [per_device(): pl.pallas_call(functools.partial(main_kernel, n, nb, part, step, names),...]
    another operation x0 -> x1, local copies, waits for them, and re-layouts: none -> 1.26 us
where the time goes in v1:
time: 57.7 us; the launch traced here: 57.4 us
  Pallas kernels  52 us (90%)
  other arithmetic  2.23 us (4%)
  local copies, waits for them, and re-layouts  1.88 us (3%)
  between operations  1.29 us (2%)
    pallas_call x1, Pallas kernels, per_device(): pl.pallas_call(functools.partial(main_kernel, n, nb, part, step, names),...  52 us
    convert_element_type x1, other arithmetic, per_device(): return (difference[None], weight_grad.astype(f32))  2.23 us
    another operation x1, local copies, waits for them, and re-layouts  1.26 us

profile of v1, /device:TPU:0, one launch (start us, length us, event | category | flops | bytes accessed | tf_op | source)
XLA Modules:
  0.0 57.4 jit_solution(7567096173387951694)
XLA Ops:
  1.3 1.3 %jit_solution_.3.refs_1_ = f32[16,128]{1,0:T(8,128)} broadcast(f32[128]{0:T(128)} %constant.2.clone), dimensions={1} | broadcast | bytes 8704 | tf_op jit(solution)
  2.5 52.0 %shard_map.212 = (f32[64,128]{1,0:T(8,128)}, bf16[64,5120]{1,0:T(8,128)(2,1)}) custom-call(s32[1]{0:T(128)S(6)} %copy.24.refs_0_, f32[16,128]{1,0:T(8,128)} %jit_solution_.3.refs_1_, bf16[3,32,5120]{2,1,0:T(8,128)(2,1)} %bitcast.6, bf16[3,32,5120]{2,1,0:T(8,128)(2,1)} %bitcast.7, bf16[128,5120]{1,0:T(8,128)(2,1)} %bitcast.5, bf16[64,5120]{1,0:T(8,128)(2,1)} %refs_5_.1, ...), custom_call_target="tpu_custom_call" | custom-call | tf_op jit(solution)/shard_map/pallas_call | solution.py:553
  54.5 0.0 copy-start
  54.5 2.2 %convert_element_type.3 = f32[64,5120]{1,0:T(8,128)} convert(bf16[64,5120]{1,0:T(8,128)(2,1)} %get-tuple-element.5) | non-fusion elementwise | flops 327680 | bytes 1966080 | tf_op jit(solution)/shard_map/convert_element_type | solution.py:563
  56.8 0.0 copy-done
  56.8 0.6 %copy.25 = f32[1,64,128]{2,1,0:T(8,128)} copy(f32[1,64,128]{2,1,0:T(8,128)S(1)} %bitcast.8) | data formatting | bytes 65536
Async XLA Ops:
  54.5 2.2 %copy-start = (f32[64,128]{1,0:T(8,128)S(1)}, f32[64,128]{1,0:T(8,128)}, u32[]{:S(2)}) copy-start(f32[64,128]{1,0:T(8,128)} %get-tuple-element.4) | copy-start | bytes 98308

commit v2 on v1

--- a/solution.py
+++ b/solution.py
@@ -79,6 +79,13 @@
     return high, (wide - high.astype(f32)).astype(bf16)
 
 
+def repeat(steps, body):
+    if steps == 1:
+        body(0, 0)
+    else:
+        lax.fori_loop(0, steps, body, 0)
+
+
 def dot_nt(left, right):
     return lax.dot_general(left, right, (((1,), (1,)), ((), ())), preferred_element_type=f32)
 
@@ -88,7 +95,7 @@
 
 
 LOADS = (
-    "timesteps", "freqs", "time0", "time1", "hidden", "gen", "noise", "embed0", "proj0", "embed1",
+    "freqs", "time0", "time1", "hidden", "gen", "noise", "embed0", "proj0", "embed1",
     "proj1", "query0", "key0", "query1", "key1", "value0", "out0", "value1", "out1", "gain0", "gain1",
 )
 
@@ -118,10 +125,9 @@
     def sem(name):
         return r["s_" + name], r["r_" + name]
 
-    loads["timesteps"].wait()
     loads["freqs"].wait()
     half = r["v_freqs"].shape[1]
-    time_step = jnp.full((16, half), r["v_timesteps"][0], jnp.int32).astype(f32)
+    time_step = jnp.full((16, half), r["timesteps"][0], jnp.int32).astype(f32)
     angles = time_step * r["v_freqs"][...]
     wave = jnp.concatenate([jnp.cos(angles), jnp.sin(angles)], axis=1).astype(bf16)
     raw = time_step[:8] * (1.0 / 1000.0)
@@ -169,7 +175,7 @@
         return pl.ds(pl.multiple_of(s * part, 128), part)
 
     def wide(s):
-        return pl.ds(pl.multiple_of(s * step, 128), step)
+        return slice(0, step) if steps == 1 else pl.ds(pl.multiple_of(s * step, 128), step)
 
     columns_held = r["columns"]
     pass_hidden = []
@@ -201,7 +207,7 @@
             gram[i] += dot_nt(jnp.concatenate([table, proj[:, wide(s)], ones], axis=0), table)
             return carry
 
-        lax.fori_loop(0, steps, gram_step, 0)
+        repeat(steps, gram_step)
 
     gram_of(0)
     landed(scatter)
@@ -233,7 +239,6 @@
             variance = jnp.sum(pair[:kin].astype(f32) * dot(gram_pair, pair), axis=0, keepdims=True)
             rscale[i : i + 1, at] = lax.rsqrt(jnp.maximum(variance, 0.0) + norm_floor)
     landed(collect)
-    pass_on([3, 5])
 
     left_ref, fold, fold_v, gate_fold = r["left"], r["fold"], r["fold_v"], r["gate_fold"]
     qk, squares, square_parts = r["qk"], r["squares"], r["square_parts"]
@@ -258,21 +263,23 @@
             shifts = jnp.where(
                 line == 0, shift_high.astype(f32), jnp.where(line == 1, shift_low.astype(f32), 0.0)
             ).astype(bf16)
-            left = jnp.concatenate([high, shifts], axis=0)
-            left_ref[i, :, at] = left
-            fold[i] += dot(left, jnp.concatenate([query[at, :], key[at, :]], axis=1))
+            left_ref[i, :kin, at] = high
+            left_ref[i, kin:, at] = shifts
+            fold[i] += dot(
+                left_ref[i, :, at], jnp.concatenate([query[at, :], key[at, :]], axis=1)
+            )
             return carry
 
-        lax.fori_loop(0, steps, fold_step, 0)
+        repeat(steps, fold_step)
         folded = jnp.concatenate(split(fold[i, :kin].T), axis=1)
         tail = fold[i, kin : kin + 8].T
         offset = tail[:, :1] + tail[:, 1:2]
         for at in blocks:
             full = dot(folded, stack[:, at]) * rscale[i : i + 1, at] + offset
             qk[i, :, at] = full
-            for j in range(2):
-                rows = full[j * head : (j + 1) * head]
-                squares[i, j : j + 1, at] = jnp.sum(rows * rows, axis=0, keepdims=True)
+            found = [full[j * head : (j + 1) * head] for j in range(2)]
+            found = [jnp.sum(rows * rows, axis=0, keepdims=True) for rows in found]
+            squares[i, :, at] = jnp.concatenate(found, axis=0).astype(squares.dtype)
         copies = exchange(
             "tm", n, lambda peer: squares.at[i], square_parts.at[i], *sem(f"sums{i}")
         )
@@ -295,7 +302,7 @@
             gate_fold[i] += dot_nt(out[:, at], (proj[:, at].astype(f32) * gate).astype(bf16))
             return carry
 
-        lax.fori_loop(0, steps, value_step, 0)
+        repeat(steps, value_step)
         gate_high, gate_low = split(gate_fold[i].T)
         value_high, value_low = split(fold_v[i])
         both = dot_nt(jnp.concatenate([gate_high, gate_low], axis=0), value_high)
@@ -307,8 +314,10 @@
             values[i, :patch_rows, at] = full.astype(bf16)
             values[i, patch_rows:, at] = jnp.ones((16, block), bf16)
 
-    sums = [fold_qk(0), fold_qk(1)]
-    pass_on([6, 7, *range(8, n)])
+    sums = [fold_qk(0)]
+    pass_on([3, 5])
+    sums.append(fold_qk(1))
+    pass_on([6, *range(8, n)])
     fold_values(0)
     fold_values(1)
 
@@ -318,7 +327,7 @@
 
     def attend(i):
         landed(sums[i])
-        inverse = lax.rsqrt(jnp.sum(square_parts[i], axis=0) / (head * n) + norm_floor)
+        inverse = lax.rsqrt(jnp.sum(square_parts[i].astype(f32), axis=0) / (head * n) + norm_floor)
         gain = r[f"v_gain{i}"]
         gains = gain[0:1, :] * gain[1:2, :]
         to_query = math.log2(math.e) / math.sqrt(HD)
@@ -359,6 +368,7 @@
     for name in ("gain0", "gain1"):
         loads[name].wait()
     give = [attend(0), attend(1)]
+    pass_on([7])
 
     own = stack[:, pl.ds(pl.multiple_of(me * frame, frame), frame)]
     velocity = []
@@ -443,15 +453,26 @@
             copies[hop - 1].wait_recv()
         shares.append(to_partner(partner(chip, hop, chips), hop))
     landed(shares)
-    weight_ref = r["weight"]
-    for s in range(chunks):
-        piece = grad[s % 2, s // 2]
-        weight_ref[:, s * part : (s + 1) * part] = piece.reshape(patch_rows, part)
     for copies in (
         scatter, spread, collect, pass_hidden, *sums, *give, difference_copies, gap_copies,
         across, back, *chain, shares,
     ):
         gone(copies)
+
+
+def last_kernel(part, grad_ref, difference_ref, weight_out, difference_out, wide_ref, sems):
+    patch_rows, width = wide_ref.shape
+    copies = [pltpu.make_async_copy(difference_ref, difference_out, sems.at[0])]
+    copies[0].start()
+    for s in range(width // part):
+        at = slice(s * part, (s + 1) * part)
+        wide_ref[:, at] = grad_ref[s % 2, s // 2].reshape(patch_rows, part).astype(f32)
+        copies.append(
+            pltpu.make_async_copy(wide_ref.at[:, at], weight_out.at[:, at], sems.at[s + 1])
+        )
+        copies[-1].start()
+    for copy in copies:
+        copy.wait()
 
 
 def per_device(
@@ -485,14 +506,14 @@
     while width % part:
         part += 128
     chunks = width // part
-    merge = max(m for m in range(1, chunks + 1) if chunks % m == 0 and m * part <= 1280 or m == 1)
+    merge = max(m for m in range(1, chunks + 1) if chunks % m == 0 and m * part <= 5120 or m == 1)
     step = merge * part
     chips, quarter, head = n // 2, patch_rows // nb, query_real.shape[1]
     kin = 2 * patch_rows
     half = FREQ // 2
     freqs = np.exp(-math.log(10000.0) * np.arange(half, dtype=np.float64) / half).astype(np.float32)
     inputs = dict(
-        timesteps=timesteps, freqs=jnp.asarray(np.broadcast_to(freqs, (16, half))),
+        freqs=jnp.asarray(np.broadcast_to(freqs, (16, half))),
         time0=time_real.transpose(1, 0, 2), time1=time_fake.transpose(1, 0, 2),
         hidden=hidden_states[0], gen=gen_weight, noise=noise_field[0],
         embed0=embed_real, proj0=proj_real, embed1=embed_fake, proj1=proj_fake,
@@ -502,13 +523,13 @@
     )
     vm = pltpu.VMEM
     outputs = dict(
-        difference=jax.ShapeDtypeStruct((patch_rows, frame), f32),
-        weight=jax.ShapeDtypeStruct((patch_rows, width), bf16),
+        difference=vm((patch_rows, frame), f32),
+        grad=vm((2, chips, nb, quarter, part), bf16),
     )
     scratch = {}
     for name in LOADS:
         array = inputs[name]
-        scratch["v_" + name] = (pltpu.SMEM if name == "timesteps" else vm)(array.shape, array.dtype)
+        scratch["v_" + name] = vm(array.shape, array.dtype)
     scratch.update(
         load_sem=pltpu.SemaphoreType.DMA((len(LOADS),)),
         patches=vm((n, patch_rows, frame), bf16),
@@ -525,8 +546,8 @@
         fold_v=vm((2, kin + 16, head), f32),
         gate_fold=vm((2, head, patch_rows), f32),
         qk=vm((2, 2 * head, tokens), f32),
-        squares=vm((2, 2, tokens), f32),
-        square_parts=vm((2, n, 2, tokens), f32),
+        squares=vm((2, 2, tokens), bf16),
+        square_parts=vm((2, n, 2, tokens), bf16),
         values=vm((2, patch_rows + 16, tokens), bf16),
         keys=vm((2, tokens, head), bf16),
         queries=vm((2, head, tokens), bf16),
@@ -539,7 +560,6 @@
         mixed=vm((nb, quarter, part), bf16),
         quarters=vm((nb, quarter, part), bf16),
         merged=vm((nb, quarter, part), bf16),
-        grad=vm((2, chips, nb, quarter, part), bf16),
     )
     for name, count in dict(
         scatter=n, spread=n, collect=n, sums0=n, sums1=n, give0=n, give1=n, diff=n, gap=n,
@@ -549,18 +569,30 @@
         scratch["r_" + name] = pltpu.SemaphoreType.DMA((count,))
     scratch["s_pass"] = pltpu.SemaphoreType.DMA((n,))
     scratch["r_pass"] = pltpu.SemaphoreType.DMA((n,))
-    names = (*inputs, *outputs, *scratch)
-    difference, weight_grad = pl.pallas_call(
+    names = ("timesteps", *LOADS, *outputs, *scratch)
+    difference, grad = pl.pallas_call(
         functools.partial(main_kernel, n, nb, part, step, names),
         out_shape=list(outputs.values()),
-        in_specs=[pl.BlockSpec(memory_space=pl.ANY)] * len(inputs),
+        in_specs=[pl.BlockSpec(memory_space=pltpu.SMEM)]
+        + [pl.BlockSpec(memory_space=pltpu.HBM)] * len(LOADS),
         out_specs=[pl.BlockSpec(memory_space=pltpu.VMEM)] * 2,
         scratch_shapes=list(scratch.values()),
         compiler_params=pltpu.CompilerParams(
             collective_id=0, has_side_effects=True, vmem_limit_bytes=60 * 1024 * 1024
         ),
-    )(*inputs.values())
-    return (difference[None], weight_grad.astype(f32))
+    )(timesteps, *(pltpu.with_memory_space_constraint(inputs[x], pltpu.HBM) for x in LOADS))
+    weight_grad, difference = pl.pallas_call(
+        functools.partial(last_kernel, part),
+        out_shape=[
+            jax.ShapeDtypeStruct((patch_rows, width), f32),
+            jax.ShapeDtypeStruct((patch_rows, frame), f32),
+        ],
+        in_specs=[pl.BlockSpec(memory_space=pltpu.VMEM)] * 2,
+        out_specs=[pl.BlockSpec(memory_space=pl.ANY)] * 2,
+        scratch_shapes=[vm((patch_rows, width), f32), pltpu.SemaphoreType.DMA((chunks + 1,))],
+        compiler_params=pltpu.CompilerParams(vmem_limit_bytes=8 * 1024 * 1024),
+    )(*(pltpu.with_memory_space_constraint(x, pltpu.VMEM) for x in (grad, difference)))
+    return (difference[None], weight_grad)
 
 
 def solution(mesh):

time: 57.7 us -> 52 us (0.901)
  Pallas kernels: 52 us -> 49.2 us
  other arithmetic: 2.23 us -> 0 us
  local copies, waits for them, and re-layouts: 1.88 us -> 1.26 us
    pallas_call x1, Pallas kernels: 52 us -> 48.1 us  [per_device(): pl.pallas_call(functools.partial(main_kernel, n, nb, part, step, names),...]
    convert_element_type x1 -> x0, other arithmetic: 2.23 us -> none  [per_device(): return (difference[None], weight_grad.astype(f32))]
    pallas_call x0 -> x1, Pallas kernels: none -> 1.14 us  [per_device(): pl.pallas_call(functools.partial(last_kernel, part), out_shape=[jax.Shape...]
    unnamed x3 -> x0, local copies, waits for them, and re-layouts: 0.62 us -> none
where the time goes in v2:
time: 52 us; the launch traced here: 51.7 us
  Pallas kernels  49.2 us (95%)
  between operations  1.28 us (2%)
  local copies, waits for them, and re-layouts  1.26 us (2%)
    pallas_call x1, Pallas kernels, per_device(): pl.pallas_call(functools.partial(main_kernel, n, nb, part, step, names),...  48.1 us
    another operation x1, local copies, waits for them, and re-layouts  1.26 us
    pallas_call x1, Pallas kernels, per_device(): pl.pallas_call(functools.partial(last_kernel, part), out_shape=[jax.Shape...  1.14 us

profile of v2, /device:TPU:0, one launch (start us, length us, event | category | flops | bytes accessed | tf_op | source)
XLA Modules:
  0.0 51.7 jit_solution(18446166228580569532)
XLA Ops:
  1.3 1.3 %jit_solution_.3.refs_1_ = f32[16,128]{1,0:T(8,128)} broadcast(f32[128]{0:T(128)} %constant.2.clone), dimensions={1} | broadcast | bytes 8704 | tf_op jit(solution)
  2.5 48.1 %shard_map.212 = (f32[64,128]{1,0:T(8,128)S(1)}, bf16[2,4,4,16,640]{4,3,2,1,0:T(8,128)(2,1)S(1)}) custom-call(s32[1]{0:T(128)S(6)} %copy.23.refs_0_, f32[16,128]{1,0:T(8,128)} %jit_solution_.3.refs_1_, bf16[3,32,5120]{2,1,0:T(8,128)(2,1)} %bitcast.6, bf16[3,32,5120]{2,1,0:T(8,128)(2,1)} %bitcast.7, bf16[128,5120]{1,0:T(8,128)(2,1)} %bitcast.5, ...), custom_call_target="tpu_custom_call" | custom-call | tf_op jit(solution)/shard_map/pallas_call | solution.py:573
  50.6 1.1 %shard_map.213 = (f32[64,5120]{1,0:T(8,128)}, f32[64,128]{1,0:T(8,128)}) custom-call(bf16[2,4,4,16,640]{4,3,2,1,0:T(8,128)(2,1)S(1)} %get-tuple-element.6.grad_ref, f32[64,128]{1,0:T(8,128)S(1)} %get-tuple-element.7.difference_ref), custom_call_target="tpu_custom_call" | custom-call | tf_op jit(solution)/shard_map/pallas_call | solution.py:584

commit v3 on v2

--- a/solution.py
+++ b/solution.py
@@ -3,7 +3,6 @@
 
 import jax
 import jax.numpy as jnp
-import numpy as np
 from jax import lax
 from jax.experimental import pallas as pl
 from jax.experimental.pallas import tpu as pltpu
@@ -46,32 +45,43 @@
     return peer
 
 
-def exchange(axis, size, source, slots, send, recv, hops=None):
-    me = lax.axis_index(axis)
-    copies = []
-    for k in hops or range(1, size):
-        peer = partner(me, k, size)
-        copy = pltpu.make_async_remote_copy(
-            src_ref=source(peer),
-            dst_ref=slots.at[me],
-            send_sem=send.at[k],
-            recv_sem=recv.at[k],
-            device_id={axis: peer},
+class Exchange:
+    def __init__(self, axis, size, source, slots, sems):
+        self.axis, self.size, self.source, self.slots, self.sems = axis, size, source, slots, sems
+
+    def start(self, hops=None):
+        me = lax.axis_index(self.axis)
+        for k in hops or range(1, self.size):
+            if k < self.size:
+                peer = partner(me, k, self.size)
+                self.copy(self.source(peer), self.slots.at[me], peer).start()
+        return self
+
+    def copy(self, source, target, peer):
+        return pltpu.make_async_remote_copy(
+            src_ref=source,
+            dst_ref=target,
+            send_sem=self.sems[0].at[0],
+            recv_sem=self.sems[1].at[0],
+            device_id={self.axis: peer},
             device_id_type=MESH,
         )
-        copy.start()
-        copies.append(copy)
-    return copies
+
+    def all(self):
+        both = self.slots.at[pl.ds(0, self.size - 1)]
+        return self.copy(both, both, lax.axis_index(self.axis))
+
+
+def exchange(axis, size, source, slots, sems):
+    return Exchange(axis, size, source, slots, sems).start()
 
 
 def landed(copies):
-    for copy in copies:
-        copy.wait_recv()
+    copies.all().wait_recv()
 
 
 def gone(copies):
-    for copy in copies:
-        copy.wait_send()
+    copies.all().wait_send()
 
 
 def split(wide):
@@ -95,7 +105,7 @@
 
 
 LOADS = (
-    "freqs", "time0", "time1", "hidden", "gen", "noise", "embed0", "proj0", "embed1",
+    "time0", "time1", "hidden", "gen", "noise", "embed0", "proj0", "embed1",
     "proj1", "query0", "key0", "query1", "key1", "value0", "out0", "value1", "out1", "gain0", "gain1",
 )
 
@@ -125,10 +135,15 @@
     def sem(name):
         return r["s_" + name], r["r_" + name]
 
-    loads["freqs"].wait()
-    half = r["v_freqs"].shape[1]
+    half = FREQ // 2
     time_step = jnp.full((16, half), r["timesteps"][0], jnp.int32).astype(f32)
-    angles = time_step * r["v_freqs"][...]
+    place = lax.broadcasted_iota(jnp.int32, (16, half), 1)
+    angles = time_step
+    bit = 1
+    while bit < half:
+        factor = math.exp(-math.log(10000.0) * bit / half)
+        angles = angles * jnp.where(lax.rem(lax.div(place, bit), 2) == 1, factor, 1.0)
+        bit *= 2
     wave = jnp.concatenate([jnp.cos(angles), jnp.sin(angles)], axis=1).astype(bf16)
     raw = time_step[:8] * (1.0 / 1000.0)
     level = ((5.0 * raw) / (1.0 + 4.0 * raw))[:1, :1]
@@ -157,7 +172,7 @@
         else:
             share_ref[s] = jnp.zeros((8, part), share_ref.dtype)
     meet({"tm": n, "batch": nb})
-    scatter = exchange("tm", n, lambda peer: share_ref.at[peer], parts, *sem("scatter"))
+    scatter = exchange("tm", n, lambda peer: share_ref.at[peer], parts, sem("scatter"))
     parts[me] = share_ref[me]
 
     loads["hidden"].wait()
@@ -167,7 +182,7 @@
     noisy = ((1.0 - level) * made + level * r["v_noise"][...].astype(f32)).astype(bf16)
     noisy_ref[...] = noisy
     patches = r["patches"]
-    spread = exchange("tm", n, lambda peer: noisy_ref, patches, *sem("spread"))
+    spread = exchange("tm", n, lambda peer: noisy_ref, patches, sem("spread"))
     patches[me] = noisy_ref[...]
     noisy = noisy.astype(f32)
 
@@ -178,18 +193,10 @@
         return slice(0, step) if steps == 1 else pl.ds(pl.multiple_of(s * step, 128), step)
 
     columns_held = r["columns"]
-    pass_hidden = []
-
-    def pass_on(hops):
-        hops = [k for k in hops if k < n]
-        if hops:
-            pass_hidden.extend(
-                exchange(
-                    "tm", n, lambda peer: hidden.at[:, columns(lax.rem(peer, chunks))],
-                    columns_held, *sem("pass"), hops,
-                )
-            )
-
+    pass_hidden = Exchange(
+        "tm", n, lambda peer: hidden.at[:, columns(lax.rem(peer, chunks))], columns_held, sem("pass")
+    )
+    pass_on = pass_hidden.start
     pass_on([1])
 
     gram = r["gram"]
@@ -212,7 +219,7 @@
     gram_of(0)
     landed(scatter)
     modul[me] = jnp.sum(parts[...].astype(f32), axis=0).astype(modul.dtype)
-    collect = exchange("tm", n, lambda peer: modul.at[me], modul, *sem("collect"))
+    collect = exchange("tm", n, lambda peer: modul.at[me], modul, sem("collect"))
     pass_on([2, 4])
     columns_held[me] = hidden[:, columns(lax.rem(me, chunks))]
     gram_of(1)
@@ -281,7 +288,7 @@
             found = [jnp.sum(rows * rows, axis=0, keepdims=True) for rows in found]
             squares[i, :, at] = jnp.concatenate(found, axis=0).astype(squares.dtype)
         copies = exchange(
-            "tm", n, lambda peer: squares.at[i], square_parts.at[i], *sem(f"sums{i}")
+            "tm", n, lambda peer: squares.at[i], square_parts.at[i], sem(f"sums{i}")
         )
         square_parts[i, me] = squares[i]
         return copies
@@ -360,7 +367,7 @@
             else:
                 lax.fori_loop(group * per_group, (group + 1) * per_group, block_step, 0)
         copies = exchange(
-            "tm", n, lambda peer: terms.at[i, peer], term_parts.at[i], *sem(f"give{i}")
+            "tm", n, lambda peer: terms.at[i, peer], term_parts.at[i], sem(f"give{i}")
         )
         term_parts[i, me] = terms[i, me]
         return copies
@@ -383,11 +390,11 @@
     difference = pred_fake - pred_real
     rounded, all_rounded, gap, gaps = r["rounded"], r["all_rounded"], r["gap"], r["gaps"]
     rounded[...] = difference.astype(bf16)
-    difference_copies = exchange("tm", n, lambda peer: rounded, all_rounded, *sem("diff"))
+    difference_copies = exchange("tm", n, lambda peer: rounded, all_rounded, sem("diff"))
     distance = jnp.abs(made - pred_real)
     distance = jnp.sum(jnp.sum(distance, axis=0, keepdims=True), axis=1, keepdims=True)
     gap[...] = jnp.broadcast_to(distance, gap.shape)
-    gap_copies = exchange("tm", n, lambda peer: gap, gaps, *sem("gap"))
+    gap_copies = exchange("tm", n, lambda peer: gap, gaps, sem("gap"))
     gaps[me] = gap[...]
     all_rounded[me] = rounded[...]
     landed(pass_hidden)
@@ -403,61 +410,63 @@
     total = total * (1.0 / (normalizer[:1, :1] * math.sqrt(nb * tokens)))
     mixed, quarters, merged, grad = r["mixed"], r["quarters"], r["merged"], r["grad"]
     mixed[...] = total.reshape(mixed.shape).astype(bf16)
-    across = exchange("batch", nb, lambda peer: mixed.at[peer], quarters, *sem("across"))
+    across = exchange("batch", nb, lambda peer: mixed.at[peer], quarters, sem("across"))
     quarters[mine] = mixed[mine]
     landed(across)
     merged[mine] = jnp.sum(quarters[...].astype(f32), axis=0).astype(bf16)
-    back = exchange("batch", nb, lambda peer: merged.at[mine], merged, *sem("back"))
-
     grad[core, chip, mine] = merged[mine]
-    chain = []
-
-    def to_chips(piece, k):
-        copies = []
+
+    def send(name, source, target, at, where):
+        copy = pltpu.make_async_remote_copy(
+            src_ref=source,
+            dst_ref=target,
+            send_sem=r["s_" + name].at[0],
+            recv_sem=r["r_" + name].at[at],
+            device_id=where,
+            device_id_type=MESH,
+        )
+        return copy
+
+    back = []
+    for k in range(1, nb):
+        back.append(
+            send("back", merged.at[mine], merged.at[mine], k, {"batch": partner(mine, k, nb)})
+        )
+        back[-1].start()
+
+    def to_chips(piece):
         for hop in range(1, chips):
-            peer = partner(chip, hop, chips)
-            copy = pltpu.make_async_remote_copy(
-                src_ref=merged.at[piece],
-                dst_ref=grad.at[core, chip, piece],
-                send_sem=r["s_chain"].at[k * chips + hop],
-                recv_sem=r["r_chain"].at[k * chips + hop],
-                device_id={"tm": 2 * peer + core},
-                device_id_type=MESH,
-            )
-            copy.start()
-            copies.append(copy)
-        return copies
-
-    chain.append(to_chips(mine, 0))
+            where = {"tm": 2 * partner(chip, hop, chips) + core}
+            send("chain", merged.at[piece], grad.at[core, chip, piece], hop, where).start()
+
+    to_chips(mine)
     for k in range(1, nb):
         back[k - 1].wait_recv()
         piece = partner(mine, k, nb)
         grad[core, chip, piece] = merged[piece]
-        chain.append(to_chips(piece, k))
-
-    def to_partner(at, hop):
-        copy = pltpu.make_async_remote_copy(
-            src_ref=grad.at[core, at],
-            dst_ref=grad.at[core, at],
-            send_sem=r["s_share"].at[hop],
-            recv_sem=r["r_share"].at[hop],
-            device_id={"tm": me + 1 - 2 * core},
-            device_id_type=MESH,
-        )
-        copy.start()
-        return copy
-
-    shares = [to_partner(chip, 0)]
+        to_chips(piece)
+
+    other = {"tm": me + 1 - 2 * core}
+
+    def to_partner(at):
+        send("share", grad.at[core, at], grad.at[core, at], 0, other).start()
+
+    to_partner(chip)
     for hop in range(1, chips):
-        for copies in chain:
-            copies[hop - 1].wait_recv()
-        shares.append(to_partner(partner(chip, hop, chips), hop))
-    landed(shares)
+        at = partner(chip, hop, chips)
+        send("chain", grad.at[core, at], grad.at[core, at], hop, other).wait_recv()
+        to_partner(at)
+    whole = send("share", grad.at[core], grad.at[1 - core], 0, other)
+    whole.wait_recv()
     for copies in (
-        scatter, spread, collect, pass_hidden, *sums, *give, difference_copies, gap_copies,
-        across, back, *chain, shares,
+        scatter, spread, collect, pass_hidden, *sums, *give, difference_copies, gap_copies, across,
     ):
         gone(copies)
+    rest = merged.at[pl.ds(0, nb - 1)]
+    send("back", rest, rest, 0, other).wait_send()
+    for hop in range(1, chips):
+        send("chain", merged, merged, 0, other).wait_send()
+    whole.wait_send()
 
 
 def last_kernel(part, grad_ref, difference_ref, weight_out, difference_out, wide_ref, sems):
@@ -510,10 +519,7 @@
     step = merge * part
     chips, quarter, head = n // 2, patch_rows // nb, query_real.shape[1]
     kin = 2 * patch_rows
-    half = FREQ // 2
-    freqs = np.exp(-math.log(10000.0) * np.arange(half, dtype=np.float64) / half).astype(np.float32)
     inputs = dict(
-        freqs=jnp.asarray(np.broadcast_to(freqs, (16, half))),
         time0=time_real.transpose(1, 0, 2), time1=time_fake.transpose(1, 0, 2),
         hidden=hidden_states[0], gen=gen_weight, noise=noise_field[0],
         embed0=embed_real, proj0=proj_real, embed1=embed_fake, proj1=proj_fake,
@@ -562,13 +568,11 @@
         merged=vm((nb, quarter, part), bf16),
     )
     for name, count in dict(
-        scatter=n, spread=n, collect=n, sums0=n, sums1=n, give0=n, give1=n, diff=n, gap=n,
-        across=nb, back=nb, chain=nb * chips, share=chips,
+        scatter=1, spread=1, collect=1, sums0=1, sums1=1, give0=1, give1=1, diff=1, gap=1,
+        across=1, back=nb, chain=chips, share=1, **{"pass": 1},
     ).items():
-        scratch["s_" + name] = pltpu.SemaphoreType.DMA((count,))
+        scratch["s_" + name] = pltpu.SemaphoreType.DMA((1,))
         scratch["r_" + name] = pltpu.SemaphoreType.DMA((count,))
-    scratch["s_pass"] = pltpu.SemaphoreType.DMA((n,))
-    scratch["r_pass"] = pltpu.SemaphoreType.DMA((n,))
     names = ("timesteps", *LOADS, *outputs, *scratch)
     difference, grad = pl.pallas_call(
         functools.partial(main_kernel, n, nb, part, step, names),

time: 52 us -> 49 us (0.942)
  Pallas kernels: 49.2 us -> 47.6 us
  local copies, waits for them, and re-layouts: 1.26 us -> 0 us
    pallas_call x1, Pallas kernels: 48.1 us -> 46.5 us  [per_device(): pl.pallas_call(functools.partial(main_kernel, n, nb, part, step, names),...]
    another operation x1 -> x0, local copies, waits for them, and re-layouts: 1.26 us -> none
where the time goes in v3:
time: 49 us; the launch traced here: 48.9 us
  Pallas kernels  47.6 us (97%)
  between operations  1.29 us (3%)
    pallas_call x1, Pallas kernels, per_device(): pl.pallas_call(functools.partial(main_kernel, n, nb, part, step, names),...  46.5 us
    pallas_call x1, Pallas kernels, per_device(): pl.pallas_call(functools.partial(last_kernel, part), out_shape=[jax.Shape...  1.14 us

profile of v3, /device:TPU:0, one launch (start us, length us, event | category | flops | bytes accessed | tf_op | source)
XLA Modules:
  0.0 48.9 jit_solution(1326265847856670031)
XLA Ops:
  1.3 46.5 %shard_map.203 = (f32[64,128]{1,0:T(8,128)S(1)}, bf16[2,4,4,16,640]{4,3,2,1,0:T(8,128)(2,1)S(1)}) custom-call(s32[1]{0:T(128)S(6)} %copy.22.refs_0_, bf16[3,32,5120]{2,1,0:T(8,128)(2,1)} %bitcast.6, bf16[3,32,5120]{2,1,0:T(8,128)(2,1)} %bitcast.7, bf16[128,5120]{1,0:T(8,128)(2,1)} %bitcast.5, bf16[64,5120]{1,0:T(8,128)(2,1)} %refs_4_.1, ...), custom_call_target="tpu_custom_call" | custom-call | tf_op jit(solution)/shard_map/pallas_call | solution.py:577
  47.8 1.1 %shard_map.204 = (f32[64,5120]{1,0:T(8,128)}, f32[64,128]{1,0:T(8,128)}) custom-call(bf16[2,4,4,16,640]{4,3,2,1,0:T(8,128)(2,1)S(1)} %get-tuple-element.6.grad_ref, f32[64,128]{1,0:T(8,128)S(1)} %get-tuple-element.7.difference_ref), custom_call_target="tpu_custom_call" | custom-call | tf_op jit(solution)/shard_map/pallas_call | solution.py:588

commit v4 on v3

--- a/solution.py
+++ b/solution.py
@@ -89,13 +89,6 @@
     return high, (wide - high.astype(f32)).astype(bf16)
 
 
-def repeat(steps, body):
-    if steps == 1:
-        body(0, 0)
-    else:
-        lax.fori_loop(0, steps, body, 0)
-
-
 def dot_nt(left, right):
     return lax.dot_general(left, right, (((1,), (1,)), ((), ())), preferred_element_type=f32)
 
@@ -110,20 +103,19 @@
 )
 
 
-def main_kernel(n, nb, part, step, names, *refs):
+def main_kernel(n, nb, part, names, *refs):
     r = dict(zip(names, refs, strict=True))
     me = lax.axis_index("tm")
     mine = lax.axis_index("batch")
     core, chip = lax.rem(me, 2), lax.div(me, 2)
     chips = n // 2
-    hidden, stack, modul = r["v_hidden"], r["stack"], r["modul"]
+    hidden, stack = r["v_hidden"], r["stack"]
     noisy_ref = r["noisy"]
     patch_rows, frame = noisy_ref.shape
     tokens = n * frame
     kin = 2 * patch_rows
     width = hidden.shape[1]
     chunks = width // part
-    steps, merge = width // step, step // part
     head = r["v_query0"].shape[1]
     freq_rows = r["v_time0"].shape[1]
     loads = {}
@@ -151,13 +143,16 @@
     column = lax.rem(lax.broadcasted_iota(jnp.int32, picked, 1), freq_rows) + me * freq_rows
     chosen = (lax.broadcasted_iota(jnp.int32, picked, 0) == column).astype(f32).astype(bf16)
     own_wave = dot(wave, chosen)
+    own_wave = jnp.concatenate([own_wave, own_wave], axis=0)
     block_of = lax.broadcasted_iota(jnp.int32, own_wave.shape, 1) // freq_rows
     row_of = lax.broadcasted_iota(jnp.int32, own_wave.shape, 0)
     share = None
     for i in (0, 1):
         loads[f"time{i}"].wait()
         table = r[f"v_time{i}"]
-        left = jnp.where(row_of == block_of + 3 * i, own_wave, 0.0).astype(bf16)
+        early = (row_of // 8 == i) & (lax.rem(row_of, 2) == block_of)
+        late = (row_of // 8 == 2) & (lax.rem(row_of, 2) == i) & (block_of == 2)
+        left = jnp.where(early | late, own_wave, 0.0).astype(bf16)
         if freq_rows % 16:
             for j in range(3):
                 term = dot(left[:, j * freq_rows : (j + 1) * freq_rows], table[j])
@@ -165,15 +160,23 @@
         else:
             term = dot(left, table[...].reshape(3 * freq_rows, width))
             share = term if share is None else share + term
-    share_ref, parts = r["share"], r["parts"]
-    for s in range(n):
-        if s < chunks:
-            share_ref[s] = share[:8, s * part : (s + 1) * part].astype(share_ref.dtype)
-        else:
-            share_ref[s] = jnp.zeros((8, part), share_ref.dtype)
+    pieces, piece_parts = r["pieces"], r["piece_parts"]
+    some = width // 4
+    line = lax.broadcasted_iota(jnp.int32, (8, some), 0) // 2
+    for g in range(3):
+        rows = share[8 * g : 8 * g + 8]
+        picked = rows[:, :some]
+        for q in range(1, 4):
+            picked = jnp.where(line == q, rows[:, q * some : (q + 1) * some], picked)
+        pieces[g] = picked.astype(bf16)
     meet({"tm": n, "batch": nb})
-    scatter = exchange("tm", n, lambda peer: share_ref.at[peer], parts, sem("scatter"))
-    parts[me] = share_ref[me]
+
+    def hand_on(g):
+        copies = exchange("tm", n, lambda peer: pieces.at[g], piece_parts.at[g], sem(f"piece{g}"))
+        piece_parts[g, me] = pieces[g]
+        return copies
+
+    piece_copies = [hand_on(0)]
 
     loads["hidden"].wait()
     loads["gen"].wait()
@@ -184,20 +187,27 @@
     patches = r["patches"]
     spread = exchange("tm", n, lambda peer: noisy_ref, patches, sem("spread"))
     patches[me] = noisy_ref[...]
+    piece_copies.extend([hand_on(1), hand_on(2)])
     noisy = noisy.astype(f32)
 
     def columns(s):
         return pl.ds(pl.multiple_of(s * part, 128), part)
 
-    def wide(s):
-        return slice(0, step) if steps == 1 else pl.ds(pl.multiple_of(s * step, 128), step)
-
-    columns_held = r["columns"]
-    pass_hidden = Exchange(
-        "tm", n, lambda peer: hidden.at[:, columns(lax.rem(peer, chunks))], columns_held, sem("pass")
-    )
-    pass_on = pass_hidden.start
-    pass_on([1])
+    held = r["held"]
+    other = {"tm": me + 1 - 2 * core}
+
+    def send(name, source, target, at, where, slot=0):
+        return pltpu.make_async_remote_copy(
+            src_ref=source,
+            dst_ref=target,
+            send_sem=r["s_" + name].at[slot],
+            recv_sem=r["r_" + name].at[at],
+            device_id=where,
+            device_id_type=MESH,
+        )
+
+    def part_of(q, side):
+        return columns(lax.rem(2 * q + side, chunks))
 
     gram = r["gram"]
     extra = kin + patch_rows
@@ -206,78 +216,46 @@
         embed, proj = r[f"v_embed{i}"], r[f"v_proj{i}"]
         loads[f"embed{i}"].wait()
         loads[f"proj{i}"].wait()
-        gram[i] = jnp.zeros(gram.shape[1:], f32)
-        ones = jnp.ones((16, step), bf16)
-
-        def gram_step(s, carry):
-            table = embed[:, wide(s)]
-            gram[i] += dot_nt(jnp.concatenate([table, proj[:, wide(s)], ones], axis=0), table)
-            return carry
-
-        repeat(steps, gram_step)
+        ones = jnp.ones((16, width), bf16)
+        gram[i] = dot_nt(jnp.concatenate([embed[...], proj[...], ones], axis=0), embed[...])
 
     gram_of(0)
-    landed(scatter)
-    modul[me] = jnp.sum(parts[...].astype(f32), axis=0).astype(modul.dtype)
-    collect = exchange("tm", n, lambda peer: modul.at[me], modul, sem("collect"))
-    pass_on([2, 4])
-    columns_held[me] = hidden[:, columns(lax.rem(me, chunks))]
+    for q in range(chips):
+        send("held", hidden.at[:, part_of(q, 1 - core)], held.at[q], 0, other).start()
     gram_of(1)
 
-    landed(spread)
-    for s in range(n):
-        at = slice(s * frame, (s + 1) * frame)
-        now = patches[s]
-        before = patches[s - 1] if s else jnp.zeros_like(now)
-        both = jnp.concatenate([now, before], axis=0)
-        stack[:kin, at] = both
-        stack[kin:, at] = both
     block = 2 * frame
     blocks = [slice(s * block, (s + 1) * block) for s in range(tokens // block)]
     rscale = r["rscale"]
-    means = []
+    means, centered = [], []
     for i in (0, 1):
         mean_row = gram[i, extra : extra + 8] / width
         means.append(mean_row.T[:, :1])
-        centered = gram[i, :kin] / width - means[i] * mean_row[:1]
-        gram_pair = jnp.concatenate(split(centered), axis=1)
-        for at in blocks:
-            pair = stack[:, at]
-            variance = jnp.sum(pair[:kin].astype(f32) * dot(gram_pair, pair), axis=0, keepdims=True)
-            rscale[i : i + 1, at] = lax.rsqrt(jnp.maximum(variance, 0.0) + norm_floor)
-    landed(collect)
+        centered.append(gram[i, :kin] / width - means[i] * mean_row[:1])
 
     left_ref, fold, fold_v, gate_fold = r["left"], r["fold"], r["fold_v"], r["gate_fold"]
     qk, squares, square_parts = r["qk"], r["squares"], r["square_parts"]
-
-    def rows_of(s, first, count):
-        found = [modul[s * merge + g].astype(f32)[first : first + count] for g in range(merge)]
-        return found[0] if merge == 1 else jnp.concatenate(found, axis=1)
 
     def fold_qk(i):
         embed, query, key = r[f"v_embed{i}"], r[f"v_query{i}"], r[f"v_key{i}"]
         loads[f"query{i}"].wait()
         loads[f"key{i}"].wait()
-        fold[i] = jnp.zeros(fold.shape[1:], f32)
-        line = lax.broadcasted_iota(jnp.int32, (16, step), 0)
-
-        def fold_step(s, carry):
-            at = wide(s)
-            rows = rows_of(s, 3 * i, 2)
-            shift, scale = rows[:1], rows[1:2]
-            high = ((embed[:, at].astype(f32) - means[i]) * (1.0 + scale)).astype(bf16)
+        landed(piece_copies[i])
+        modul = jnp.sum(piece_parts[i].astype(f32), axis=0)
+        line = lax.broadcasted_iota(jnp.int32, (16, some), 0)
+        for q in range(4):
+            at = slice(q * some, (q + 1) * some)
+            shift, scale = modul[2 * q : 2 * q + 1], modul[2 * q + 1 : 2 * q + 2]
+            left_ref[i, :kin, at] = (
+                (embed[:, at].astype(f32) - means[i]) * (1.0 + scale)
+            ).astype(bf16)
             shift_high, shift_low = split(shift)
-            shifts = jnp.where(
+            left_ref[i, kin:, at] = jnp.where(
                 line == 0, shift_high.astype(f32), jnp.where(line == 1, shift_low.astype(f32), 0.0)
             ).astype(bf16)
-            left_ref[i, :kin, at] = high
-            left_ref[i, kin:, at] = shifts
-            fold[i] += dot(
-                left_ref[i, :, at], jnp.concatenate([query[at, :], key[at, :]], axis=1)
-            )
-            return carry
-
-        repeat(steps, fold_step)
+        fold[i] = dot(left_ref[i], jnp.concatenate([query[...], key[...]], axis=1))
+
+    def project_qk(i):
         folded = jnp.concatenate(split(fold[i, :kin].T), axis=1)
         tail = fold[i, kin : kin + 8].T
         offset = tail[:, :1] + tail[:, 1:2]
@@ -295,21 +273,21 @@
 
     values = r["values"]
 
-    def fold_values(i):
-        value, out, proj = r[f"v_value{i}"], r[f"v_out{i}"], r[f"v_proj{i}"]
+    def fold_value(i):
         loads[f"value{i}"].wait()
+        fold_v[i] = dot(left_ref[i], r[f"v_value{i}"][...])
+
+    def fold_gate(i):
+        out, proj = r[f"v_out{i}"], r[f"v_proj{i}"]
         loads[f"out{i}"].wait()
-        fold_v[i] = jnp.zeros(fold_v.shape[1:], f32)
-        gate_fold[i] = jnp.zeros(gate_fold.shape[1:], f32)
-
-        def value_step(s, carry):
-            at = wide(s)
-            gate = rows_of(s, 3 * i + 2, 1)
-            fold_v[i] += dot(left_ref[i, :, at], value[at, :])
-            gate_fold[i] += dot_nt(out[:, at], (proj[:, at].astype(f32) * gate).astype(bf16))
-            return carry
-
-        repeat(steps, value_step)
+        gated = []
+        for q in range(4):
+            at = slice(q * some, (q + 1) * some)
+            gate = gate_sum[2 * q + i : 2 * q + i + 1]
+            gated.append((proj[:, at].astype(f32) * gate).astype(bf16))
+        gate_fold[i] = dot_nt(out[...], jnp.concatenate(gated, axis=1))
+
+    def join(i):
         gate_high, gate_low = split(gate_fold[i].T)
         value_high, value_low = split(fold_v[i])
         both = dot_nt(jnp.concatenate([gate_high, gate_low], axis=0), value_high)
@@ -321,20 +299,43 @@
             values[i, :patch_rows, at] = full.astype(bf16)
             values[i, patch_rows:, at] = jnp.ones((16, block), bf16)
 
-    sums = [fold_qk(0)]
-    pass_on([3, 5])
-    sums.append(fold_qk(1))
-    pass_on([6, *range(8, n)])
-    fold_values(0)
-    fold_values(1)
+    fold_qk(0)
+    landed(spread)
+    for s in range(n):
+        at = slice(s * frame, (s + 1) * frame)
+        now = patches[s]
+        before = patches[s - 1] if s else jnp.zeros_like(now)
+        both = jnp.concatenate([now, before], axis=0)
+        stack[:kin, at] = both
+        stack[kin:, at] = both
+    for i in (0, 1):
+        gram_pair = jnp.concatenate(split(centered[i]), axis=1)
+        for at in blocks:
+            pair = stack[:, at]
+            variance = jnp.sum(pair[:kin].astype(f32) * dot(gram_pair, pair), axis=0, keepdims=True)
+            rscale[i : i + 1, at] = lax.rsqrt(jnp.maximum(variance, 0.0) + norm_floor)
+    sums = [project_qk(0)]
+    fold_value(0)
+    fold_qk(1)
+    sums.append(project_qk(1))
+    fold_value(1)
+    landed(piece_copies[2])
+    gate_sum = jnp.sum(piece_parts[2].astype(f32), axis=0)
+    fold_gate(0)
+    fold_gate(1)
+    join(0)
+    join(1)
 
     groups = min(4, tokens // block)
     per_group = tokens // block // groups
     keys, terms, term_parts = r["keys"], r["terms"], r["term_parts"]
 
-    def attend(i):
-        landed(sums[i])
-        inverse = lax.rsqrt(jnp.sum(square_parts[i].astype(f32), axis=0) / (head * n) + norm_floor)
+    starts = [block * b * (b + 1) // 2 for b in range(tokens // block)]
+
+    def prepare(i):
+        inverse = lax.rsqrt(
+            jnp.sum(square_parts[i].astype(f32), axis=0) / (head * n) + norm_floor
+        )
         gain = r[f"v_gain{i}"]
         gains = gain[0:1, :] * gain[1:2, :]
         to_query = math.log2(math.e) / math.sqrt(HD)
@@ -342,6 +343,34 @@
             gained = qk[i, head:, at] * inverse[1:2, at]
             keys[i, at, :] = (gained.T * gains).astype(bf16)
             r["queries"][i, :, at] = (qk[i, :head, at] * (inverse[:1, at] * to_query)).astype(bf16)
+
+    def put(i, b, powers, length):
+        summed = dot(values[i, :, :length], powers)
+        term = (summed[:patch_rows] / summed[patch_rows : patch_rows + 1]).astype(bf16)
+        for j in range(2):
+            terms[i, 2 * b + j] = term[:, j * frame : (j + 1) * frame]
+
+    def score(i):
+        early = lax.broadcasted_iota(jnp.int32, (frame, block), 1) < frame
+        for b, (at, start) in enumerate(zip(blocks, starts)):
+            length = (b + 1) * block
+            scores = dot(keys[i, :length], r["queries"][i, :, at])
+            r["scores"][i, start : start + length - frame] = scores[: length - frame]
+            edge = jnp.where(early, -1e30, scores[length - frame :])
+            r["scores"][i, start + length - frame : start + length] = edge
+
+    def soften(i):
+        for b, start in enumerate(starts):
+            rows = slice(start, start + (b + 1) * block)
+            peak = jnp.max(r["scores"][i, rows], axis=0, keepdims=True)
+            r["powers"][i, rows] = jnp.exp2(r["scores"][i, rows] - peak).astype(bf16)
+
+    def combine(i):
+        for b, start in enumerate(starts):
+            length = (b + 1) * block
+            put(i, b, r["powers"][i, start : start + length], length)
+
+    def looped(i):
         for group in range(groups):
             length = (group + 1) * per_group * block
             low = length - per_group * block
@@ -355,17 +384,12 @@
                 edge = jnp.where(key_frame <= query_frame, scores[low:], -1e30)
                 scores = jnp.concatenate([scores[:low], edge], axis=0) if low else edge
                 peak = jnp.max(scores, axis=0, keepdims=True)
-                powers = jnp.exp2(scores - peak).astype(bf16)
-                summed = dot(values[i, :, :length], powers)
-                term = (summed[:patch_rows] / summed[patch_rows : patch_rows + 1]).astype(bf16)
-                for j in range(2):
-                    terms[i, 2 * b + j] = term[:, j * frame : (j + 1) * frame]
+                put(i, b, jnp.exp2(scores - peak).astype(bf16), length)
                 return carry
 
-            if per_group == 1:
-                block_step(group, 0)
-            else:
-                lax.fori_loop(group * per_group, (group + 1) * per_group, block_step, 0)
+            lax.fori_loop(group * per_group, (group + 1) * per_group, block_step, 0)
+
+    def hand_out(i):
         copies = exchange(
             "tm", n, lambda peer: terms.at[i, peer], term_parts.at[i], sem(f"give{i}")
         )
@@ -374,8 +398,17 @@
 
     for name in ("gain0", "gain1"):
         loads[name].wait()
-    give = [attend(0), attend(1)]
-    pass_on([7])
+    give = []
+    for i in (0, 1):
+        landed(sums[i])
+        prepare(i)
+        if per_group == 1:
+            score(i)
+            soften(i)
+            combine(i)
+        else:
+            looped(i)
+        give.append(hand_out(i))
 
     own = stack[:, pl.ds(pl.multiple_of(me * frame, frame), frame)]
     velocity = []
@@ -388,45 +421,55 @@
     pred_real = noisy - level * velocity[0]
     pred_fake = noisy - level * velocity[1]
     difference = pred_fake - pred_real
-    rounded, all_rounded, gap, gaps = r["rounded"], r["all_rounded"], r["gap"], r["gaps"]
+    rounded, rounded_other, gap, gaps = r["rounded"], r["rounded_other"], r["gap"], r["gaps"]
     rounded[...] = difference.astype(bf16)
-    difference_copies = exchange("tm", n, lambda peer: rounded, all_rounded, sem("diff"))
+    swap = send("swap", rounded, rounded_other, 0, other)
+    swap.start()
     distance = jnp.abs(made - pred_real)
     distance = jnp.sum(jnp.sum(distance, axis=0, keepdims=True), axis=1, keepdims=True)
     gap[...] = jnp.broadcast_to(distance, gap.shape)
     gap_copies = exchange("tm", n, lambda peer: gap, gaps, sem("gap"))
     gaps[me] = gap[...]
-    all_rounded[me] = rounded[...]
-    landed(pass_hidden)
-    landed(difference_copies)
-    total = None
-    for s in range(0, n, 2):
-        lefts = jnp.concatenate([all_rounded[s], all_rounded[s + 1]], axis=1)
-        term = dot(lefts, columns_held[s : s + 2].reshape(2 * frame, part))
-        total = term if total is None else total + term
+    products, partial, gathered = r["products"], r["partial"], r["gathered"]
+    hops = [*range(chips - 1, 0, -1), 0]
+    for hop in hops:
+        products[hop] = dot(rounded[...], hidden[:, part_of(partner(chip, hop, chips), core)])
+    all_held = send("held", held, held, 0, other)
+    all_held.wait_recv()
+    swap.wait_recv()
+    order = [*range(nb - 1, 0, -1), 0]
+    for hop in hops:
+        at = partner(chip, hop, chips)
+        whole = products[hop] + dot(rounded_other[...], held[at])
+        partial[hop] = whole.reshape(partial.shape[1:]).astype(bf16)
+    for k in order:
+        piece = partner(mine, k, nb)
+        for hop in hops[:-1]:
+            where = {"tm": 2 * partner(chip, hop, chips) + core}
+            send("plane", partial.at[hop, piece], gathered.at[k, hop], k, where).start()
     landed(gap_copies)
     normalizer = jnp.maximum(jnp.sum(gaps[...], axis=0) / (patch_rows * tokens), gap_floor)
     r["difference"][...] = difference / normalizer[:1, :1]
-    total = total * (1.0 / (normalizer[:1, :1] * math.sqrt(nb * tokens)))
+    factor = 1.0 / (normalizer[:1, :1] * math.sqrt(nb * tokens))
     mixed, quarters, merged, grad = r["mixed"], r["quarters"], r["merged"], r["grad"]
-    mixed[...] = total.reshape(mixed.shape).astype(bf16)
-    across = exchange("batch", nb, lambda peer: mixed.at[peer], quarters, sem("across"))
-    quarters[mine] = mixed[mine]
-    landed(across)
+    for k in order:
+        piece = partner(mine, k, nb)
+        near = gathered.at[k, pl.ds(1, chips - 1)]
+        send("plane", near, near, k, other).wait_recv()
+        summed = partial[0, piece].astype(f32)
+        for hop in hops[:-1]:
+            summed = summed + gathered[k, hop].astype(f32)
+        summed = (summed * factor).astype(bf16)
+        if k:
+            mixed[k] = summed
+            send("across", mixed.at[k], quarters.at[k], 0, {"batch": piece}).start()
+        else:
+            quarters[0] = summed
+    far = quarters.at[pl.ds(1, nb - 1)]
+    across = send("across", far, far, 0, other)
+    across.wait_recv()
     merged[mine] = jnp.sum(quarters[...].astype(f32), axis=0).astype(bf16)
     grad[core, chip, mine] = merged[mine]
-
-    def send(name, source, target, at, where):
-        copy = pltpu.make_async_remote_copy(
-            src_ref=source,
-            dst_ref=target,
-            send_sem=r["s_" + name].at[0],
-            recv_sem=r["r_" + name].at[at],
-            device_id=where,
-            device_id_type=MESH,
-        )
-        return copy
-
     back = []
     for k in range(1, nb):
         back.append(
@@ -445,8 +488,6 @@
         piece = partner(mine, k, nb)
         grad[core, chip, piece] = merged[piece]
         to_chips(piece)
-
-    other = {"tm": me + 1 - 2 * core}
 
     def to_partner(at):
         send("share", grad.at[core, at], grad.at[core, at], 0, other).start()
@@ -459,9 +500,15 @@
     whole = send("share", grad.at[core], grad.at[1 - core], 0, other)
     whole.wait_recv()
     for copies in (
-        scatter, spread, collect, pass_hidden, *sums, *give, difference_copies, gap_copies, across,
+        *piece_copies, spread, *sums, *give, gap_copies,
     ):
         gone(copies)
+    all_held.wait_send()
+    swap.wait_send()
+    for k in order:
+        near = gathered.at[k, pl.ds(1, chips - 1)]
+        send("plane", near, near, k, other).wait_send()
+    across.wait_send()
     rest = merged.at[pl.ds(0, nb - 1)]
     send("back", rest, rest, 0, other).wait_send()
     for hop in range(1, chips):
@@ -515,8 +562,8 @@
     while width % part:
         part += 128
     chunks = width // part
-    merge = max(m for m in range(1, chunks + 1) if chunks % m == 0 and m * part <= 5120 or m == 1)
-    step = merge * part
+    many = tokens // (2 * frame)
+    held_rows = many * (many + 1) * frame if many <= 4 else 16
     chips, quarter, head = n // 2, patch_rows // nb, query_real.shape[1]
     kin = 2 * patch_rows
     inputs = dict(
@@ -539,11 +586,13 @@
     scratch.update(
         load_sem=pltpu.SemaphoreType.DMA((len(LOADS),)),
         patches=vm((n, patch_rows, frame), bf16),
-        share=vm((n, 8, part), bf16),
-        parts=vm((n, 8, part), bf16),
-        modul=vm((n, 8, part), bf16),
+        pieces=vm((3, 8, width // 4), bf16),
+        piece_parts=vm((3, n, 8, width // 4), bf16),
         noisy=vm((patch_rows, frame), bf16),
-        columns=vm((n, frame, part), bf16),
+        held=vm((chips, frame, part), bf16),
+        products=vm((chips, patch_rows, part), f32),
+        partial=vm((chips, nb, quarter, part), bf16),
+        gathered=vm((nb, chips, quarter, part), bf16),
         gram=vm((2, kin + patch_rows + 16, kin), f32),
         stack=vm((2 * kin, tokens), bf16),
         rscale=vm((2, tokens), f32),
@@ -557,25 +606,27 @@
         values=vm((2, patch_rows + 16, tokens), bf16),
         keys=vm((2, tokens, head), bf16),
         queries=vm((2, head, tokens), bf16),
+        scores=vm((2, held_rows, 2 * frame), f32),
+        powers=vm((2, held_rows, 2 * frame), bf16),
         terms=vm((2, n, patch_rows, frame), bf16),
         term_parts=vm((2, n, patch_rows, frame), bf16),
         gap=vm((8, 128), f32),
         gaps=vm((n, 8, 128), f32),
         rounded=vm((patch_rows, frame), bf16),
-        all_rounded=vm((n, patch_rows, frame), bf16),
+        rounded_other=vm((patch_rows, frame), bf16),
         mixed=vm((nb, quarter, part), bf16),
         quarters=vm((nb, quarter, part), bf16),
         merged=vm((nb, quarter, part), bf16),
     )
     for name, count in dict(
-        scatter=1, spread=1, collect=1, sums0=1, sums1=1, give0=1, give1=1, diff=1, gap=1,
-        across=1, back=nb, chain=chips, share=1, **{"pass": 1},
+        piece0=1, piece1=1, piece2=1, spread=1, sums0=1, sums1=1, give0=1, give1=1, gap=1,
+        held=1, swap=1, plane=nb, across=1, back=nb, chain=chips, share=1,
     ).items():
         scratch["s_" + name] = pltpu.SemaphoreType.DMA((1,))
         scratch["r_" + name] = pltpu.SemaphoreType.DMA((count,))
     names = ("timesteps", *LOADS, *outputs, *scratch)
     difference, grad = pl.pallas_call(
-        functools.partial(main_kernel, n, nb, part, step, names),
+        functools.partial(main_kernel, n, nb, part, names),
         out_shape=list(outputs.values()),
         in_specs=[pl.BlockSpec(memory_space=pltpu.SMEM)]
         + [pl.BlockSpec(memory_space=pltpu.HBM)] * len(LOADS),

time: 49 us -> 44.8 us (0.914)
  Pallas kernels: 47.6 us -> 43.3 us
    pallas_call x1, Pallas kernels: 46.5 us -> 42.2 us  [per_device(): pl.pallas_call(functools.partial(main_kernel, n, nb, part, names), out_sh...]
where the time goes in v4:
time: 44.8 us; the launch traced here: 44.6 us
  Pallas kernels  43.3 us (97%)
  between operations  1.29 us (3%)
    pallas_call x1, Pallas kernels, per_device(): pl.pallas_call(functools.partial(main_kernel, n, nb, part, names), out_sh...  42.2 us
    pallas_call x1, Pallas kernels, per_device(): pl.pallas_call(functools.partial(last_kernel, part), out_shape=[jax.Shape...  1.14 us

profile of v4, /device:TPU:0, one launch (start us, length us, event | category | flops | bytes accessed | tf_op | source)
XLA Modules:
  0.0 44.6 jit_solution(3019779052240707711)
XLA Ops:
  1.3 42.2 %shard_map.203 = (f32[64,128]{1,0:T(8,128)S(1)}, bf16[2,4,4,16,640]{4,3,2,1,0:T(8,128)(2,1)S(1)}) custom-call(s32[1]{0:T(128)S(6)} %copy.22.refs_0_, bf16[3,32,5120]{2,1,0:T(8,128)(2,1)} %bitcast.6, bf16[3,32,5120]{2,1,0:T(8,128)(2,1)} %bitcast.7, bf16[128,5120]{1,0:T(8,128)(2,1)} %bitcast.5, bf16[64,5120]{1,0:T(8,128)(2,1)} %refs_4_.1, ...), custom_call_target="tpu_custom_call" | custom-call | tf_op jit(solution)/shard_map/pallas_call | solution.py:628
  43.5 1.1 %shard_map.204 = (f32[64,5120]{1,0:T(8,128)}, f32[64,128]{1,0:T(8,128)}) custom-call(bf16[2,4,4,16,640]{4,3,2,1,0:T(8,128)(2,1)S(1)} %get-tuple-element.6.grad_ref, f32[64,128]{1,0:T(8,128)S(1)} %get-tuple-element.7.difference_ref), custom_call_target="tpu_custom_call" | custom-call | tf_op jit(solution)/shard_map/pallas_call | solution.py:639

commit v5 on v4

--- a/solution.py
+++ b/solution.py
@@ -49,12 +49,11 @@
     def __init__(self, axis, size, source, slots, sems):
         self.axis, self.size, self.source, self.slots, self.sems = axis, size, source, slots, sems
 
-    def start(self, hops=None):
+    def start(self):
         me = lax.axis_index(self.axis)
-        for k in hops or range(1, self.size):
-            if k < self.size:
-                peer = partner(me, k, self.size)
-                self.copy(self.source(peer), self.slots.at[me], peer).start()
+        for k in range(self.size - 1, 0, -1):
+            peer = partner(me, k, self.size)
+            self.copy(self.source(peer), self.slots.at[me], peer).start()
         return self
 
     def copy(self, source, target, peer):
@@ -238,8 +237,6 @@
 
     def fold_qk(i):
         embed, query, key = r[f"v_embed{i}"], r[f"v_query{i}"], r[f"v_key{i}"]
-        loads[f"query{i}"].wait()
-        loads[f"key{i}"].wait()
         landed(piece_copies[i])
         modul = jnp.sum(piece_parts[i].astype(f32), axis=0)
         line = lax.broadcasted_iota(jnp.int32, (16, some), 0)
@@ -274,12 +271,10 @@
     values = r["values"]
 
     def fold_value(i):
-        loads[f"value{i}"].wait()
         fold_v[i] = dot(left_ref[i], r[f"v_value{i}"][...])
 
     def fold_gate(i):
         out, proj = r[f"v_out{i}"], r[f"v_proj{i}"]
-        loads[f"out{i}"].wait()
         gated = []
         for q in range(4):
             at = slice(q * some, (q + 1) * some)
@@ -299,7 +294,11 @@
             values[i, :patch_rows, at] = full.astype(bf16)
             values[i, patch_rows:, at] = jnp.ones((16, block), bf16)
 
+    loads["query0"].wait()
+    loads["key0"].wait()
     fold_qk(0)
+    for name in LOADS[LOADS.index("query1") :]:
+        loads[name].wait()
     landed(spread)
     for s in range(n):
         at = slice(s * frame, (s + 1) * frame)
@@ -396,8 +395,6 @@
         term_parts[i, me] = terms[i, me]
         return copies
 
-    for name in ("gain0", "gain1"):
-        loads[name].wait()
     give = []
     for i in (0, 1):
         landed(sums[i])
@@ -475,10 +472,12 @@
         back.append(
             send("back", merged.at[mine], merged.at[mine], k, {"batch": partner(mine, k, nb)})
         )
-        back[-1].start()
+
+    for copy in back[::-1]:
+        copy.start()
 
     def to_chips(piece):
-        for hop in range(1, chips):
+        for hop in range(chips - 1, 0, -1):
             where = {"tm": 2 * partner(chip, hop, chips) + core}
             send("chain", merged.at[piece], grad.at[core, chip, piece], hop, where).start()
 

time: 44.8 us -> 43.7 us (0.975)
  Pallas kernels: 43.3 us -> 42.2 us
    pallas_call x1, Pallas kernels: 42.2 us -> 41.1 us  [per_device(): pl.pallas_call(functools.partial(main_kernel, n, nb, part, names), out_sh...]
where the time goes in v5:
time: 43.7 us; the launch traced here: 43.5 us
  Pallas kernels  42.2 us (97%)
  between operations  1.29 us (3%)
    pallas_call x1, Pallas kernels, per_device(): pl.pallas_call(functools.partial(main_kernel, n, nb, part, names), out_sh...  41.1 us
    pallas_call x1, Pallas kernels, per_device(): pl.pallas_call(functools.partial(last_kernel, part), out_shape=[jax.Shape...  1.14 us

profile of v5, /device:TPU:0, one launch (start us, length us, event | category | flops | bytes accessed | tf_op | source)
XLA Modules:
  0.0 43.5 jit_solution(7676506132157054994)
XLA Ops:
  1.3 41.1 %shard_map.203 = (f32[64,128]{1,0:T(8,128)S(1)}, bf16[2,4,4,16,640]{4,3,2,1,0:T(8,128)(2,1)S(1)}) custom-call(s32[1]{0:T(128)S(6)} %copy.22.refs_0_, bf16[3,32,5120]{2,1,0:T(8,128)(2,1)} %bitcast.6, bf16[3,32,5120]{2,1,0:T(8,128)(2,1)} %bitcast.7, bf16[128,5120]{1,0:T(8,128)(2,1)} %bitcast.5, bf16[64,5120]{1,0:T(8,128)(2,1)} %refs_4_.1, ...), custom_call_target="tpu_custom_call" | custom-call | tf_op jit(solution)/shard_map/pallas_call | solution.py:627
  42.4 1.1 %shard_map.204 = (f32[64,5120]{1,0:T(8,128)}, f32[64,128]{1,0:T(8,128)}) custom-call(bf16[2,4,4,16,640]{4,3,2,1,0:T(8,128)(2,1)S(1)} %get-tuple-element.6.grad_ref, f32[64,128]{1,0:T(8,128)S(1)} %get-tuple-element.7.difference_ref), custom_call_target="tpu_custom_call" | custom-call | tf_op jit(solution)/shard_map/pallas_call | solution.py:638

commit v6 on v5

--- a/solution.py
+++ b/solution.py
@@ -317,13 +317,6 @@
     fold_value(0)
     fold_qk(1)
     sums.append(project_qk(1))
-    fold_value(1)
-    landed(piece_copies[2])
-    gate_sum = jnp.sum(piece_parts[2].astype(f32), axis=0)
-    fold_gate(0)
-    fold_gate(1)
-    join(0)
-    join(1)
 
     groups = min(4, tokens // block)
     per_group = tokens // block // groups
@@ -395,12 +388,25 @@
         term_parts[i, me] = terms[i, me]
         return copies
 
+    fold_value(1)
+    landed(piece_copies[2])
+    gate_sum = jnp.sum(piece_parts[2].astype(f32), axis=0)
+    landed(sums[0])
+    fold_gate(0)
+    fold_gate(1)
+    prepare(0)
+    if per_group == 1:
+        score(0)
+    join(0)
+    join(1)
     give = []
     for i in (0, 1):
-        landed(sums[i])
-        prepare(i)
+        if i:
+            landed(sums[i])
+            prepare(i)
         if per_group == 1:
-            score(i)
+            if i:
+                score(i)
             soften(i)
             combine(i)
         else:
@@ -476,26 +482,24 @@
     for copy in back[::-1]:
         copy.start()
 
-    def to_chips(piece):
+    def to_chips(piece, k):
         for hop in range(chips - 1, 0, -1):
             where = {"tm": 2 * partner(chip, hop, chips) + core}
-            send("chain", merged.at[piece], grad.at[core, chip, piece], hop, where).start()
-
-    to_chips(mine)
+            target = grad.at[core, chip, piece]
+            send("chain", merged.at[piece], target, k * chips + hop, where).start()
+        send("share", merged.at[piece], grad.at[core, chip, piece], 0, other).start()
+
+    to_chips(mine, 0)
     for k in range(1, nb):
         back[k - 1].wait_recv()
         piece = partner(mine, k, nb)
         grad[core, chip, piece] = merged[piece]
-        to_chips(piece)
-
-    def to_partner(at):
-        send("share", grad.at[core, at], grad.at[core, at], 0, other).start()
-
-    to_partner(chip)
-    for hop in range(1, chips):
-        at = partner(chip, hop, chips)
-        send("chain", grad.at[core, at], grad.at[core, at], hop, other).wait_recv()
-        to_partner(at)
+        to_chips(piece, k)
+    for k in range(nb):
+        for hop in range(1, chips):
+            slot = grad.at[core, partner(chip, hop, chips), partner(mine, k, nb)]
+            send("chain", slot, slot, k * chips + hop, other).wait_recv()
+            send("share", slot, slot, 0, other).start()
     whole = send("share", grad.at[core], grad.at[1 - core], 0, other)
     whole.wait_recv()
     for copies in (
@@ -619,7 +623,7 @@
     )
     for name, count in dict(
         piece0=1, piece1=1, piece2=1, spread=1, sums0=1, sums1=1, give0=1, give1=1, gap=1,
-        held=1, swap=1, plane=nb, across=1, back=nb, chain=chips, share=1,
+        held=1, swap=1, plane=nb, across=1, back=nb, chain=nb * chips, share=1,
     ).items():
         scratch["s_" + name] = pltpu.SemaphoreType.DMA((1,))
         scratch["r_" + name] = pltpu.SemaphoreType.DMA((count,))

time: 43.7 us -> 43.2 us (0.989)
  Pallas kernels: 42.2 us -> 41.7 us
    pallas_call x1, Pallas kernels: 41.1 us -> 40.6 us  [per_device(): pl.pallas_call(functools.partial(main_kernel, n, nb, part, names), out_sh...]
where the time goes in v6:
time: 43.2 us; the launch traced here: 43 us
  Pallas kernels  41.7 us (97%)
  between operations  1.29 us (3%)
    pallas_call x1, Pallas kernels, per_device(): pl.pallas_call(functools.partial(main_kernel, n, nb, part, names), out_sh...  40.6 us
    pallas_call x1, Pallas kernels, per_device(): pl.pallas_call(functools.partial(last_kernel, part), out_shape=[jax.Shape...  1.14 us

profile of v6, /device:TPU:0, one launch (start us, length us, event | category | flops | bytes accessed | tf_op | source)
XLA Modules:
  0.0 43.0 jit_solution(3943812194732197693)
XLA Ops:
  1.3 40.6 %shard_map.203 = (f32[64,128]{1,0:T(8,128)S(1)}, bf16[2,4,4,16,640]{4,3,2,1,0:T(8,128)(2,1)S(1)}) custom-call(s32[1]{0:T(128)S(6)} %copy.22.refs_0_, bf16[3,32,5120]{2,1,0:T(8,128)(2,1)} %bitcast.6, bf16[3,32,5120]{2,1,0:T(8,128)(2,1)} %bitcast.7, bf16[128,5120]{1,0:T(8,128)(2,1)} %bitcast.5, bf16[64,5120]{1,0:T(8,128)(2,1)} %refs_4_.1, ...), custom_call_target="tpu_custom_call" | custom-call | tf_op jit(solution)/shard_map/pallas_call | solution.py:631
  41.9 1.1 %shard_map.204 = (f32[64,5120]{1,0:T(8,128)}, f32[64,128]{1,0:T(8,128)}) custom-call(bf16[2,4,4,16,640]{4,3,2,1,0:T(8,128)(2,1)S(1)} %get-tuple-element.6.grad_ref, f32[64,128]{1,0:T(8,128)S(1)} %get-tuple-element.7.difference_ref), custom_call_target="tpu_custom_call" | custom-call | tf_op jit(solution)/shard_map/pallas_call | solution.py:642
